TPU v7x, 128 devices: a whole 4x4x4 slice. The times are simulated.
128 devices in a mesh: lat: 8 (over z, core), lon: 16 (over y, x).
Axes of the slice: x: 4, y: 4, z: 4, core: 2. Of those that a mesh axis runs over, the one named last changes fastest.
Arguments:
- zonal_wind: float32 [32, 64, 2048], P(None, 'lat', 'lon'), may hold values from -6 to 6
- merid_wind: float32 [32, 64, 2048], P(None, 'lat', 'lon'), may hold values from -6 to 6
- vertical_wind: float32 [32, 64, 2048], P(None, 'lat', 'lon'), may hold values from -6 to 6
- pressure: float32 [32, 64, 2048], P(None, 'lat', 'lon'), may hold values from -6 to 6
- zonal_coef: float32 [64], P('lat'), may hold values from 0.05 to 0.4
- merid_coef: float32 [64], P('lat'), may hold values from 0.05 to 0.4
- level_coef: float32 [32], replicated, may hold values from 0.3 to 1.5
- sound_coef: float32 [32, 64, 2048], P(None, 'lat', 'lon'), may hold values from 0.2 to 2
- cutoff: int32 [64], replicated, may hold values from 1 to 511
- filter_mask: int32 [64], replicated, may hold values from 0 to 1, as said below
Outputs:
- zonal_next: float32 [32, 64, 2048], P(None, 'lat', 'lon')
- merid_next: float32 [32, 64, 2048], P(None, 'lat', 'lon')
- vertical_next: float32 [32, 64, 2048], P(None, 'lat', 'lon')
- pressure_next: float32 [32, 64, 2048], P(None, 'lat', 'lon')
Inputs may be any that keep to these rules, and one draw needn't show every extreme that they name: `filter_mask`: for every latitude j below 32 exactly one of j and j + 32 is filtered; the filtered ones are the first n and the last 32 - n latitudes, for some n from 8 to 24.
All inputs are finite; a program needn't handle non-finite values.
Results may differ from a plain program's by a relative error of at most 0.0001.
Values sent between devices are 32-bit elements; how exact they have to be, the bound alone decides.
A program may use at most 64 MiB of HBM per device.

v0:
```python
import math

import jax
import jax.numpy as jnp
from jax import lax
from jax.sharding import Mesh
from jax.sharding import PartitionSpec as P

SUBSTEPS = 2
LON = ("lon_0", "lon_1")


def cut_along(value, dim, size):
    before, after = (value.shape[:dim], value.shape[dim + 1 :])
    return jnp.moveaxis(value.reshape(*before, size, -1, *after), dim, 0)


def in_order(tiles, dim):
    shape = list(tiles.shape[1:])
    shape[dim] *= tiles.shape[0]
    return jnp.moveaxis(tiles, 0, dim).reshape(shape)


def exchange_in_order(tiles, axes, turns):
    inside = tiles.shape[1:]
    out = tiles.reshape(*(lax.axis_size(a) for a in axes), *inside)
    for k in turns:
        out = lax.all_to_all(out, axes[k], k, k, tiled=True)
    return out.reshape(-1, *inside)


def stepwise_exchange(value, axes, turns, split_dim, concat_dim):
    tiles = cut_along(value, split_dim, lax.axis_size(axes))
    return in_order(exchange_in_order(tiles, axes, turns), concat_dim)


def padded_2(value, sides, width):
    edges = {}
    for axis, dim in sides:
        size, length = (lax.axis_size(axis), value.shape[dim])
        up = [(i, (i + 1) % size) for i in range(size)]
        last = lax.slice_in_dim(value, length - width, length, axis=dim)
        initial = lax.slice_in_dim(value, 0, width, axis=dim)
        edges[dim] = (
            lax.ppermute(last, axis, up),
            lax.ppermute(initial, axis, [(b, a) for a, b in up]),
        )
    done = []
    for _, dim in sides:
        low, high = edges[dim]
        around = [(width, width) if d in done else (0, 0) for d in range(value.ndim)]
        value = jnp.concatenate([jnp.pad(low, around), value, jnp.pad(high, around)], axis=dim)
        done.append(dim)
    return value


def rim_fix(padded, lat_dim):
    band_index = lax.axis_index("lat")
    bands = lax.axis_size("lat")
    extent = padded.shape[lat_dim]
    position = lax.broadcasted_iota(jnp.int32, padded.shape, lat_dim)
    first_edge = jnp.logical_and(position == 0, band_index == 0)
    final_edge = jnp.logical_and(position == extent - 1, band_index == bands - 1)
    return jnp.where(jnp.logical_or(first_edge, final_edge), 0.0, padded)


def dft_tables(length):
    half_len = length // 2
    sample = lax.broadcasted_iota(jnp.int32, (length, length), 0)
    column = lax.broadcasted_iota(jnp.int32, (length, length), 1)
    is_cosine = column <= half_len
    wavenum = jnp.where(is_cosine, column, column - half_len)
    phase = sample * wavenum % length
    angle = 2.0 * math.pi / length * phase.astype(jnp.float32)
    forward = jnp.where(is_cosine, jnp.cos(angle), jnp.sin(angle))
    single = jnp.logical_and(is_cosine, jnp.logical_or(wavenum == 0, wavenum == half_len))
    weight = jnp.where(single, 1.0, 2.0) / length
    inverse = jnp.transpose(forward * weight)
    wave_row = wavenum[0].astype(jnp.float32)
    return (forward, inverse, wave_row)


def damping(wave_row, limits):
    bound_col = limits[:, None]
    ratio = bound_col / jnp.maximum(wave_row[None, :], 1.0)
    return jnp.where(wave_row[None, :] > bound_col, ratio * ratio, 1.0)


def transform_band(block, limits, forward, inverse, wave_row):
    circles = lax.all_to_all(block, LON, split_axis=1, concat_axis=3, tiled=True)
    spectra = jnp.einsum("vetj,jc->vetc", circles, forward, precision=lax.Precision.HIGHEST)
    scaled = spectra * damping(wave_row, limits)
    damped = jnp.einsum("vetc,cj->vetj", scaled, inverse, precision=lax.Precision.HIGHEST)
    return stepwise_exchange(damped, LON, (0, 1), 3, 1)


def filtered_increments(increments, own_flags, own_limits, forward, inverse, wave_row):
    flag_cols = own_flags[:, None]
    damped = transform_band(increments, own_limits, forward, inverse, wave_row)
    return jnp.where(flag_cols, damped, increments)


def column_solve(vertical_wind, pstar, level_coef, sound_coef):
    levels = vertical_wind.shape[0]
    zero_slab = jnp.zeros_like(vertical_wind[0])
    ratios = []
    values = []
    prev_ratio = zero_slab
    prev_value = zero_slab
    for level in range(levels):
        alpha = level_coef[level]
        below = alpha * sound_coef[level]
        if level + 1 < levels:
            above = alpha * sound_coef[level + 1]
            rhs = vertical_wind[level] - alpha * (pstar[level + 1] - pstar[level])
        else:
            above = zero_slab
            rhs = vertical_wind[level] + alpha * pstar[level]
        pivot = 1.0 + below + above + below * prev_ratio
        prev_ratio = -above / pivot
        prev_value = (rhs + below * prev_value) / pivot
        ratios.append(prev_ratio)
        values.append(prev_value)
    solved = [zero_slab] * levels
    upper_value = values[levels - 1]
    solved[levels - 1] = upper_value
    for level in range(levels - 2, -1, -1):
        upper_value = values[level] - ratios[level] * upper_value
        solved[level] = upper_value
    new_wind = jnp.stack(solved)
    wind_below = jnp.concatenate([zero_slab[None], new_wind[:-1]], axis=0)
    new_pressure = pstar - sound_coef * (new_wind - wind_below)
    return (new_wind, new_pressure)


def body(
    zonal_wind,
    merid_wind,
    vertical_wind,
    pressure,
    zonal_coef,
    merid_coef,
    level_coef,
    sound_coef,
    cutoff,
    filter_mask,
):
    lat_rows = pressure.shape[1]
    start = lax.axis_index("lat") * lat_rows
    own_flags = lax.dynamic_slice_in_dim(filter_mask, start, lat_rows) > 0
    own_limits = lax.dynamic_slice_in_dim(cutoff, start, lat_rows).astype(jnp.float32)
    forward, inverse, wave_row = dft_tables(pressure.shape[2] * lax.axis_size(LON))
    zonal_rows = zonal_coef[None, :, None]
    merid_rows = merid_coef[None, :, None]
    for step in range(SUBSTEPS):
        padded = padded_2(pressure, (("lat", 1), (LON, 2)), 1)
        padded = rim_fix(padded, 1)
        zonal_step = -zonal_rows * (padded[:, 1:-1, 2:] - padded[:, 1:-1, :-2])
        merid_step = -merid_rows * (padded[:, 2:, 1:-1] - padded[:, :-2, 1:-1])
        increments = jnp.stack([zonal_step, merid_step])
        damped = filtered_increments(increments, own_flags, own_limits, forward, inverse, wave_row)
        winds = jnp.stack([zonal_wind, merid_wind]) + damped
        wind_pad = padded_2(winds, (("lat", 2), (LON, 3)), 1)
        wind_pad = rim_fix(wind_pad, 2)
        diverge = zonal_rows * (wind_pad[0, :, 1:-1, 2:] - wind_pad[0, :, 1:-1, :-2])
        diverge = diverge + merid_rows * (wind_pad[1, :, 2:, 1:-1] - wind_pad[1, :, :-2, 1:-1])
        pstar = pressure - sound_coef * diverge
        vertical_wind, pressure = column_solve(vertical_wind, pstar, level_coef, sound_coef)
        zonal_wind = winds[0]
        merid_wind = winds[1]
    return (zonal_wind, merid_wind, vertical_wind, pressure)


def solution(mesh):
    split = Mesh(mesh.devices.reshape(mesh.shape["lat"], 4, 4), ("lat", "lon_0", "lon_1"))
    in_specs = (
        P(None, "lat", LON),
        P(None, "lat", LON),
        P(None, "lat", LON),
        P(None, "lat", LON),
        P("lat"),
        P("lat"),
        P(),
        P(None, "lat", LON),
        P(),
        P(),
    )
    out_specs = (P(None, "lat", LON), P(None, "lat", LON), P(None, "lat", LON), P(None, "lat", LON))
    return jax.shard_map(body, mesh=split, in_specs=in_specs, out_specs=out_specs, check_vma=False)
```

profile of v0, /device:TPU:0, one launch (start us, length us, event | category | flops | bytes accessed | tf_op | source)
XLA Modules:
  0.0 473.1 jit_solution(12453796442951394225)
XLA Ops:
  0.7 1.1 fusion.90
  1.8 1.7 collective-permute-start
  3.5 3.8 collective-permute-start.3
  7.3 1.0 fusion.89
  8.3 3.2 collective-permute-start.2
  11.5 2.1 iota_select_fusion
  13.9 0.4 fusion.24
  14.5 0.7 copy.62
  15.2 4.0 all-to-all-start
  19.3 8.7 %all-to-all-done = f32[2,32,8,128]{3,2,0,1:T(8,128)S(1)} async-done(((f32[2,32,8,128]{3,2,0,1:T(8,128)}), f32[2,32,8,128]{3,2,0,1:T(8,128)S(1)}, u32[]{:S(2)}, u32[]{:S(2)}) %all-to-all-start) | async-done | bytes 262176 | tf_op jit(solution)/shard_map/all_to_all | solution.py:90
  28.2 75.1 %fusion.15 = f32[2,2,8,2048]{3,2,1,0:T(8,128)S(1)} fusion(f32[2,2,8,2048]{3,2,1,0:T(8,128)S(1)} %all_to_all.41, s32[2048]{0:T(1024)S(1)} %iota_add_fusion, pred[2048]{0:T(1024)(128)(4,1)S(1)} %iota_compare_fusion.4, f32[8,2048]{1,0:T(8,128)S(1)} %fusion.47), kind=kOutput, calls=%fused_computation.21 | convolution fusion | flops 1677787136 | bytes 600064 | tf_op jit(solution)/shard_map/vetj,jc->vetc/dot_general | solution.py:91
  103.3 81.4 %fusion.5 = f32[2,2,8,2048]{3,2,1,0:T(8,128)S(1)} fusion(f32[2,2,8,2048]{3,2,1,0:T(8,128)S(1)} %fusion.15, s32[2048]{0:T(1024)S(1)} %iota_add_fusion, pred[2048]{0:T(1024)(128)(4,1)S(1)} %iota_compare_fusion.4), kind=kOutput, calls=%fused_computation.8 | convolution fusion | flops 1707081728 | bytes 534528 | tf_op jit(solution)/shard_map/vetc,cj->vetj/dot_general | solution.py:93
  184.8 9.1 %all_to_all.56 = f32[4,4,2,2,8,128]{5,4,1,3,2,0:T(8,128)S(1)} all-to-all(f32[4,4,2,2,8,128]{5,4,1,3,2,0:T(8,128)S(1)} %copy.65), channel_id=1, replica_groups=mesh['lat'=8,'lon_0'=4,'lon_1'=4] {'lon_0'}, dimensions={0} | all-to-all | bytes 524288 | tf_op jit(solution)/shard_map/all_to_all | solution.py:28
  193.8 0.7 copy.66
  194.5 3.4 all-to-all-start.2
  198.1 0.7 fusion.91
  198.8 5.8 %all-to-all-done.2 = f32[4,4,2,2,8,128]{5,4,0,3,2,1:T(8,128)S(1)} async-done(((f32[4,4,2,2,8,128]{5,4,0,3,2,1:T(8,128)}), f32[4,4,2,2,8,128]{5,4,0,3,2,1:T(8,128)S(1)}, u32[]{:S(2)}, u32[]{:S(2)}) %all-to-all-start.2) | async-done | bytes 262176 | tf_op jit(solution)/shard_map/all_to_all | solution.py:28
  205.0 0.6 collective-permute-start.4
  205.6 5.2 %collective-permute-start.7 = (f32[2,32,8,1]{3,2,1,0:T(8,128)S(1)}, f32[2,32,8,1]{3,2,1,0:T(8,128)S(1)}, u32[]{:S(2)}, u32[]{:S(2)}) collective-permute-start(f32[2,32,8,1]{3,2,1,0:T(8,128)S(1)} %get-tuple-element.205), channel_id=1, source_target_pairs={{1,0},{2,1},{3,2},{4,3},{5,4},{6,5},{7,6},{8,7},{9,8},{10,9},{11,1... | collective-permute-start | bytes 6152 | tf_op jit(solution)/shard_map/ppermute | solution.py:46
  210.8 3.0 collective-permute-start.6
  213.7 0.7 fusion.92
  214.4 0.3 collective-permute-done.4
  214.7 0.6 collective-permute-done.5
  215.3 0.8 fusion.22
  216.1 0.2 fusion.40
  216.3 19.6 %add_divide_fusion.32 = (f32[1,8,128]{2,1,0:T(8,128)S(1)}, f32[1,8,128]{2,1,0:T(8,128)S(1)}, f32[1,8,128]{2,1,0:T(8,128)S(1)}, f32[1,8,128]{2,1,0:T(8,128)S(1)},...) fusion(f32[32,8,128]{2,1,0:T(8,128)S(1)} %copy-done.6, ...), kind=kLoop, calls=%fused_computation.317 | loop fusion | flops 441344 | bytes 761980 | tf_op jit(solution)/shard_map/div | solution.py:121
  235.9 1.4 constant_dynamic-update-slice_fusion.62
  237.8 3.3 collective-permute-start.10
  241.1 2.5 collective-permute-start.11
  243.6 3.3 collective-permute-done.11
  246.9 6.1 %collective-permute-done.8 = f32[32,8,1]{2,1,0:T(8,128)S(1)} collective-permute-done((f32[32,8,1]{2,1,0:T(8,128)S(1)}, f32[32,8,1]{2,1,0:T(8,128)S(1)}, u32[]{:S(2)}, u32[]{:S(2)}) %collective-permute-start.8) | collective-permute-done | bytes 1056 | tf_op jit(solution)/shard_map/ppermute | solution.py:45
  253.0 0.4 fusion.23
  253.6 11.9 %all_to_all.57 = f32[2,32,8,128]{3,2,0,1:T(8,128)S(1)} all-to-all(f32[2,32,8,128]{3,2,0,1:T(8,128)S(1)} %copy.69), channel_id=1, replica_groups=mesh['lat'=8,'lon_0'=4,'lon_1'=4] {'lon_0','lon_1'}, dimensions={1} | all-to-all | bytes 524288 | tf_op jit(solution)/shard_map/all_to_all | solution.py:90
  265.7 75.1 %fusion.18 = f32[2,2,8,2048]{3,2,1,0:T(8,128)S(1)} fusion(f32[2,2,8,2048]{3,2,1,0:T(8,128)S(1)} %all_to_all.47, s32[2048]{0:T(1024)S(1)} %iota_add_fusion, pred[2048]{0:T(1024)(128)(4,1)S(1)} %iota_compare_fusion.4, f32[8,2048]{1,0:T(8,128)S(1)} %fusion.47), kind=kOutput, calls=%fused_computation.22 | convolution fusion | flops 1677787136 | bytes 600064 | tf_op jit(solution)/shard_map/vetj,jc->vetc/dot_general | solution.py:91
  340.8 81.3 %fusion.3 = f32[2,2,8,2048]{3,2,1,0:T(8,128)S(1)} fusion(f32[2,2,8,2048]{3,2,1,0:T(8,128)S(1)} %fusion.18, s32[2048]{0:T(1024)S(1)} %iota_add_fusion, pred[2048]{0:T(1024)(128)(4,1)S(1)} %iota_compare_fusion.4), kind=kOutput, calls=%fused_computation.6 | convolution fusion | flops 1707081728 | bytes 534528 | tf_op jit(solution)/shard_map/vetc,cj->vetj/dot_general | solution.py:93
  422.2 9.1 %all_to_all.58 = f32[4,4,2,2,8,128]{5,4,1,3,2,0:T(8,128)S(1)} all-to-all(f32[4,4,2,2,8,128]{5,4,1,3,2,0:T(8,128)S(1)} %copy.72), channel_id=1, replica_groups=mesh['lat'=8,'lon_0'=4,'lon_1'=4] {'lon_0'}, dimensions={0} | all-to-all | bytes 524288 | tf_op jit(solution)/shard_map/all_to_all | solution.py:28
  431.3 9.1 %all_to_all.59 = f32[4,4,2,2,8,128]{5,4,0,3,2,1:T(8,128)S(1)} all-to-all(f32[4,4,2,2,8,128]{5,4,0,3,2,1:T(8,128)S(1)} %copy.73), channel_id=1, replica_groups=mesh['lat'=8,'lon_0'=4,'lon_1'=4] {'lon_1'}, dimensions={1} | all-to-all | bytes 524288 | tf_op jit(solution)/shard_map/all_to_all | solution.py:28
  440.7 0.6 collective-permute-start.12
  441.3 4.8 %collective-permute-start.15 = (f32[2,32,8,1]{3,2,1,0:T(8,128)S(1)}, f32[2,32,8,1]{3,2,1,0:T(8,128)S(1)}, u32[]{:S(2)}, u32[]{:S(2)}) collective-permute-start(f32[2,32,8,1]{3,2,1,0:T(8,128)S(1)} %get-tuple-element.199), channel_id=1, source_target_pairs={{1,0},{2,1},{3,2},{4,3},{5,4},{6,5},{7,6},{8,7},{9,8},{10,9},{11,1... | collective-permute-start | bytes 6152 | tf_op jit(solution)/shard_map/ppermute | solution.py:46
  446.1 3.0 collective-permute-start.14
  449.1 0.7 slice_bitcast_fusion
  449.8 0.7 collective-permute-done.12
  450.5 0.2 collective-permute-done.13
  450.7 0.8 fusion.21
  451.4 0.2 fusion.29
  451.6 19.5 %add_divide_fusion.1 = (f32[1,8,128]{2,1,0:T(8,128)S(1)}, f32[1,8,128]{2,1,0:T(8,128)S(1)}, f32[1,8,128]{2,1,0:T(8,128)S(1)}, f32[1,8,128]{2,1,0:T(8,128)S(1)}, ...) fusion(f32[1,8,128]{2,1,0:T(8,128)S(1)} %get-tuple-element.102,, ...), kind=kLoop, calls=%fused_computation.252 | loop fusion | flops 226304 | bytes 635004 | tf_op jit(solution)/shard_map/div | solution.py:121
  471.1 0.8 constant_dynamic-update-slice_fusion.125
  472.3 0.7 multiply_subtract_fusion
  (136 shorter events, 2.3 us)
Async XLA Ops:
  0.6 13.2 %copy-start.1 = (f32[32,8,128]{2,1,0:T(8,128)S(1)}, f32[32,8,128]{2,1,0:T(8,128)}, u32[]{:S(2)}) copy-start(f32[32,8,128]{2,1,0:T(8,128)} %param.13) | copy-start | bytes 393220
  0.6 13.0 %copy-start.9 = (s32[64]{0:T(128)S(1)}, s32[64]{0:T(128)}, u32[]{:S(2)}) copy-start(s32[64]{0:T(128)} %param.18) | copy-start | bytes 772
  0.7 13.1 %copy-start.7 = (f32[8]{0:T(128)S(1)}, f32[8]{0:T(128)}, u32[]{:S(2)}) copy-start(f32[8]{0:T(128)} %param.14) | copy-start | bytes 100
  0.7 13.1 %copy-start.8 = (f32[8]{0:T(128)S(1)}, f32[8]{0:T(128)}, u32[]{:S(2)}) copy-start(f32[8]{0:T(128)} %param.15) | copy-start | bytes 100
  1.8 12.0 %collective-permute-start = (f32[32,8,1]{2,1,0:T(8,128)S(1)}, f32[32,8,1]{2,1,0:T(8,128)S(1)}, u32[]{:S(2)}, u32[]{:S(2)}) collective-permute-start(f32[32,8,1]{2,1,0:T(8,128)S(1)} %get-tuple-element.212), channel_id=1, source_target_pairs={{0,1},{1,2},{2,3},{3,4},{4,5},{5,6},{6,7},{7,8},{8,9},{9,10},{10,1... | collective-permute-start | bytes 3080 | tf_op jit(solution)/shard_map/ppermute | solution.py:45
  3.5 10.4 %collective-permute-start.3 = (f32[32,8,1]{2,1,0:T(8,128)S(1)}, f32[32,8,1]{2,1,0:T(8,128)S(1)}, u32[]{:S(2)}, u32[]{:S(2)}) collective-permute-start(f32[32,8,1]{2,1,0:T(8,128)S(1)} %get-tuple-element.213), channel_id=1, source_target_pairs={{1,0},{2,1},{3,2},{4,3},{5,4},{6,5},{7,6},{8,7},{9,8},{10,9},{11,1... | collective-permute-start | bytes 3080 | tf_op jit(solution)/shard_map/ppermute | solution.py:46
  8.3 5.6 %collective-permute-start.1 = (f32[32,1,128]{2,1,0:T(1,128)S(1)}, f32[32,1,128]{2,1,0:T(1,128)S(1)}, u32[]{:S(2)}, u32[]{:S(2)}) collective-permute-start(f32[32,1,128]{2,1,0:T(1,128)S(1)} %get-tuple-element.210), channel_id=1, source_target_pairs={{0,16},{16,32},{32,48},{48,64},{64,80},{80,96},{96,112},{112,0},{1... | collective-permute-start | bytes 49160 | tf_op jit(solution)/shard_map/ppermute | solution.py:45
  8.3 5.5 %collective-permute-start.2 = (f32[32,1,128]{2,1,0:T(1,128)S(1)}, f32[32,1,128]{2,1,0:T(1,128)S(1)}, u32[]{:S(2)}, u32[]{:S(2)}) collective-permute-start(f32[32,1,128]{2,1,0:T(1,128)S(1)} %get-tuple-element.211), channel_id=1, source_target_pairs={{16,0},{32,16},{48,32},{64,48},{80,64},{96,80},{112,96},{0,112},{1... | collective-permute-start | bytes 49160 | tf_op jit(solution)/shard_map/ppermute | solution.py:46
  15.2 12.8 %all-to-all-start = ((f32[2,32,8,128]{3,2,0,1:T(8,128)}), f32[2,32,8,128]{3,2,0,1:T(8,128)S(1)}, u32[]{:S(2)}, u32[]{:S(2)}) async-start(f32[2,32,8,128]{3,2,0,1:T(8,128)} %copy.62), calls=%async_computation | async-start | bytes 524288 | tf_op jit(solution)/shard_map/all_to_all | solution.py:90
  103.2 94.7 %copy-start.10 = (s32[64]{0:T(128)S(1)}, s32[64]{0:T(128)}, u32[]{:S(2)}) copy-start(s32[64]{0:T(128)} %param.19) | copy-start | bytes 772
  103.3 94.8 %copy-start.2 = (f32[32]{0:T(128)S(1)}, f32[32]{0:T(128)}, u32[]{:S(2)}) copy-start(f32[32]{0:T(128)} %param.16) | copy-start | bytes 388
  103.3 101.4 %copy-start.3 = (f32[32,8,128]{2,1,0:T(8,128)S(1)}, f32[32,8,128]{2,1,0:T(8,128)}, u32[]{:S(2)}) copy-start(f32[32,8,128]{2,1,0:T(8,128)} %param.11) | copy-start | bytes 393220
  103.3 101.4 %copy-start.4 = (f32[32,8,128]{2,1,0:T(8,128)S(1)}, f32[32,8,128]{2,1,0:T(8,128)}, u32[]{:S(2)}) copy-start(f32[32,8,128]{2,1,0:T(8,128)} %param.10) | copy-start | bytes 393220
  103.3 112.8 %copy-start = (f32[32,8,128]{2,1,0:T(8,128)S(1)}, f32[32,8,128]{2,1,0:T(8,128)}, u32[]{:S(2)}) copy-start(f32[32,8,128]{2,1,0:T(8,128)} %param.17) | copy-start | bytes 393220
  103.3 113.0 %copy-start.6 = (f32[32,8,128]{2,1,0:T(8,128)S(1)}, f32[32,8,128]{2,1,0:T(8,128)}, u32[]{:S(2)}) copy-start(f32[32,8,128]{2,1,0:T(8,128)} %param.12) | copy-start | bytes 393220
  194.5 10.1 %all-to-all-start.2 = ((f32[4,4,2,2,8,128]{5,4,0,3,2,1:T(8,128)}), f32[4,4,2,2,8,128]{5,4,0,3,2,1:T(8,128)S(1)}, u32[]{:S(2)}, u32[]{:S(2)}) async-start(f32[4,4,2,2,8,128]{5,4,0,3,2,1:T(8,128)} %copy.66), calls=%async_computation.2 | async-start | bytes 524288 | tf_op jit(solution)/shard_map/all_to_all | solution.py:28
  205.0 9.8 %collective-permute-start.4 = (f32[2,32,8,1]{3,2,1,0:T(8,128)S(1)}, f32[2,32,8,1]{3,2,1,0:T(8,128)S(1)}, u32[]{:S(2)}, u32[]{:S(2)}) collective-permute-start(f32[2,32,8,1]{3,2,1,0:T(8,128)S(1)} %get-tuple-element.204), channel_id=1, source_target_pairs={{0,1},{1,2},{2,3},{3,4},{4,5},{5,6},{6,7},{7,8},{8,9},{9,10},{10,1... | collective-permute-start | bytes 6152 | tf_op jit(solution)/shard_map/ppermute | solution.py:45
  205.6 9.1 %collective-permute-start.7 = (f32[2,32,8,1]{3,2,1,0:T(8,128)S(1)}, f32[2,32,8,1]{3,2,1,0:T(8,128)S(1)}, u32[]{:S(2)}, u32[]{:S(2)}) collective-permute-start(f32[2,32,8,1]{3,2,1,0:T(8,128)S(1)} %get-tuple-element.205), channel_id=1, source_target_pairs={{1,0},{2,1},{3,2},{4,3},{5,4},{6,5},{7,6},{8,7},{9,8},{10,9},{11,1... | collective-permute-start | bytes 6152 | tf_op jit(solution)/shard_map/ppermute | solution.py:46
  210.8 4.6 collective-permute-start.5
  210.8 4.6 collective-permute-start.6
  237.8 15.2 %collective-permute-start.10 = (f32[32,1,128]{2,1,0:T(1,128)S(1)}, f32[32,1,128]{2,1,0:T(1,128)S(1)}, u32[]{:S(2)}, u32[]{:S(2)}) collective-permute-start(f32[32,1,128]{2,1,0:T(1,128)S(1)} %get-tuple-element.207), channel_id=1, source_target_pairs={{16,0},{32,16},{48,32},{64,48},{80,64},{96,80},{112,96},{0,112},{1... | collective-permute-start | bytes 49160 | tf_op jit(solution)/shard_map/ppermute | solution.py:46
  241.0 12.0 %collective-permute-start.9 = (f32[32,1,128]{2,1,0:T(1,128)S(1)}, f32[32,1,128]{2,1,0:T(1,128)S(1)}, u32[]{:S(2)}, u32[]{:S(2)}) collective-permute-start(f32[32,1,128]{2,1,0:T(1,128)S(1)} %get-tuple-element.206), channel_id=1, source_target_pairs={{0,16},{16,32},{32,48},{48,64},{64,80},{80,96},{96,112},{112,0},{1... | collective-permute-start | bytes 49160 | tf_op jit(solution)/shard_map/ppermute | solution.py:45
  241.1 5.8 %collective-permute-start.11 = (f32[32,8,1]{2,1,0:T(8,128)S(1)}, f32[32,8,1]{2,1,0:T(8,128)S(1)}, u32[]{:S(2)}, u32[]{:S(2)}) collective-permute-start(f32[32,8,1]{2,1,0:T(8,128)S(1)} %get-tuple-element.209), channel_id=1, source_target_pairs={{1,0},{2,1},{3,2},{4,3},{5,4},{6,5},{7,6},{8,7},{9,8},{10,9},{11,1... | collective-permute-start | bytes 3080 | tf_op jit(solution)/shard_map/ppermute | solution.py:46
  243.6 9.4 %collective-permute-start.8 = (f32[32,8,1]{2,1,0:T(8,128)S(1)}, f32[32,8,1]{2,1,0:T(8,128)S(1)}, u32[]{:S(2)}, u32[]{:S(2)}) collective-permute-start(f32[32,8,1]{2,1,0:T(8,128)S(1)} %get-tuple-element.208), channel_id=1, source_target_pairs={{0,1},{1,2},{2,3},{3,4},{4,5},{5,6},{6,7},{7,8},{8,9},{9,10},{10,1... | collective-permute-start | bytes 3080 | tf_op jit(solution)/shard_map/ppermute | solution.py:45
  440.7 9.8 %collective-permute-start.12 = (f32[2,32,8,1]{3,2,1,0:T(8,128)S(1)}, f32[2,32,8,1]{3,2,1,0:T(8,128)S(1)}, u32[]{:S(2)}, u32[]{:S(2)}) collective-permute-start(f32[2,32,8,1]{3,2,1,0:T(8,128)S(1)} %get-tuple-element.198), channel_id=1, source_target_pairs={{0,1},{1,2},{2,3},{3,4},{4,5},{5,6},{6,7},{7,8},{8,9},{9,10},{10,1... | collective-permute-start | bytes 6152 | tf_op jit(solution)/shard_map/ppermute | solution.py:45
  441.3 9.1 %collective-permute-start.15 = (f32[2,32,8,1]{3,2,1,0:T(8,128)S(1)}, f32[2,32,8,1]{3,2,1,0:T(8,128)S(1)}, u32[]{:S(2)}, u32[]{:S(2)}) collective-permute-start(f32[2,32,8,1]{3,2,1,0:T(8,128)S(1)} %get-tuple-element.199), channel_id=1, source_target_pairs={{1,0},{2,1},{3,2},{4,3},{5,4},{6,5},{7,6},{8,7},{9,8},{10,9},{11,1... | collective-permute-start | bytes 6152 | tf_op jit(solution)/shard_map/ppermute | solution.py:46
  446.1 4.6 collective-permute-start.13
  446.1 4.6 collective-permute-start.14
  472.2 0.7 copy-start.5
where the time goes:
time: 479 us; the launch traced here: 473 us
  matrix products  313 us (65%)
  other arithmetic  47.7 us (10%)
  starting transfers between devices  39 us (8%)
  blocking collectives  39 us (8%)
  waiting for transfers between devices  25.7 us (5%)
  local copies, waits for them, and re-layouts  6.99 us (1%)
    dot_general x2, matrix products, transform_band(): jnp.einsum('vetc,cj->vetj', scaled, inverse, precision=lax.Precision.HIGH...  163 us
    dot_general x2, matrix products, transform_band(): jnp.einsum('vetj,jc->vetc', circles, forward, precision=lax.Precision.HIG...  150 us
    div x2, other arithmetic, column_solve(): prev_value = (rhs + below * prev_value) / pivot  39.1 us
    ppermute x8, starting transfers between devices, padded_2(): lax.ppermute(initial, axis, [(b, a) for a, b in up])  28.6 us
    all_to_all x3, blocking collectives, exchange_in_order(): out = lax.all_to_all(out, axes[k], k, k, tiled=True)  27.2 us
    all_to_all x1, blocking collectives, transform_band(): lax.all_to_all(block, LON, split_axis=1, concat_axis=3, tiled=True)  11.9 us
  transfers between devices with their start and end apart: 18, of which 8 were waited for; matrix products, arithmetic and copies ran while one was open for 1% of the time, Pallas kernels for 0%

commit v1 on v0

v1 whole, which is shorter than its diff:
```python
import math

import jax
import jax.numpy as jnp
import numpy as np
from jax import lax
from jax.experimental import pallas as pl
from jax.experimental.pallas import tpu as pltpu
from jax.sharding import PartitionSpec as P

SUBSTEPS = 2
F32 = jnp.float32
NG = 8
ND = 16
NL = 32
MESH = pl.DeviceIdType.MESH


def tables():
    lane = np.arange(128)
    ang = 2.0 * np.pi * ((lane[:, None] * lane[None, :]) % 128) / 128.0
    c, s = np.cos(ang), np.sin(ang)
    mat = np.block([[c, -s], [s, c]]).astype(np.float32)
    tang = 2.0 * np.pi * (np.arange(16)[:, None] * lane[None, :]) / 2048.0
    tw = np.stack([np.cos(tang), -np.sin(tang)]).astype(np.float32)
    return mat, tw


def dft4(x):
    (ar, ai), (br, bi), (cr, ci), (dr, di) = x
    sr, si = ar + cr, ai + ci
    tr, ti = ar - cr, ai - ci
    ur, ui = br + dr, bi + di
    vr, vi = br - dr, bi - di
    return [(sr + ur, si + ui), (tr + vi, ti - vr), (sr - ur, si - ui), (tr - vi, ti + vr)]


def dft16(x):
    cols = []
    for n2 in range(4):
        y = dft4([x[4 * n1 + n2] for n1 in range(4)])
        out = []
        for k1 in range(4):
            e = (n2 * k1) % 16
            yr, yi = y[k1]
            if e == 0:
                out.append((yr, yi))
            elif e == 4:
                out.append((yi, -yr))
            else:
                c, s = math.cos(2 * math.pi * e / 16), math.sin(2 * math.pi * e / 16)
                out.append((yr * c + yi * s, yi * c - yr * s))
        cols.append(out)
    res = [None] * 16
    for k1 in range(4):
        z = dft4([cols[n2][k1] for n2 in range(4)])
        for k2 in range(4):
            res[k1 + 4 * k2] = z[k2]
    return res


def hops(off):
    return sum(min(o, 4 - o) for o in off)


OFFS = sorted([(a, b) for a in range(4) for b in range(4)], key=lambda o: -hops(o))


def kernel(
    zc_s, mc_s, a_s, cut_s, msk_s, u_h, v_h, w_h, p_h, s_h, mat_h, tw_h,
    uo_h, vo_h, wo_h, po_h,
    uv, vv, wv, pv, sv, mat, tw, p1, w1, p2, w2, xm, xe, bs, hs, lhs, res, dsend, back,
    du, dv, ru, rv, rat, inv, qq, div0, eu, eul, eur, ev, mct, mcp, mcn, fo, fh,
    ldsem, outsem, sendsem, fmsem, fesem, bksem, esem,
):
    me = lax.axis_index("lon")
    g = lax.axis_index("lat")
    up = (g + 1) % NG
    dn = (g + NG - 1) % NG
    my, mx = me // 4, me % 4
    east = (me + 1) % ND
    west = (me + ND - 1) % ND

    loads = [
        pltpu.make_async_copy(a, b, ldsem.at[i])
        for i, (a, b) in enumerate(
            [(p_h, pv), (u_h, uv), (v_h, vv), (s_h, sv), (w_h, wv), (tw_h, tw), (mat_h, mat)]
        )
    ]
    for c in loads:
        c.start()

    bar = pltpu.get_barrier_semaphore()

    def target(off):
        return ((my + off[0]) % 4) * 4 + (mx + off[1]) % 4

    for off in OFFS:
        d = target(off)
        pl.semaphore_signal(bar, inc=1, device_id={"lat": up, "lon": d}, device_id_type=MESH)
        pl.semaphore_signal(bar, inc=1, device_id={"lat": dn, "lon": d}, device_id_type=MESH)
        if off != (0, 0):
            pl.semaphore_signal(bar, inc=1, device_id={"lat": g, "lon": d}, device_id_type=MESH)

    def rcopy(src, dst, si, sem, gg, d):
        c = pltpu.make_async_remote_copy(
            src_ref=src, dst_ref=dst, send_sem=sendsem.at[si], recv_sem=sem,
            device_id={"lat": gg, "lon": d}, device_id_type=MESH,
        )
        c.start()

    def forward(ph, src):
        for off in OFFS:
            d = target(off)
            if off != (0, 0):
                rcopy(src.at[pl.ds(2 * d, 2)], xm.at[ph, me], 3 * ph, fmsem.at[ph], g, d)
            rcopy(src.at[pl.ds(2 * d, 2), 6:8], xe.at[ph, me, :, 6:8], 3 * ph + 1, fesem.at[ph, 0], up, d)
            rcopy(src.at[pl.ds(2 * d, 2), 0:2], xe.at[ph, me, :, 0:2], 3 * ph + 2, fesem.at[ph, 1], dn, d)
        xm[ph, pl.ds(me, 1)] = src[pl.ds(2 * me, 2)][None]

    def wait15(buf, sem):
        pltpu.make_async_copy(buf.at[pl.ds(0, 15)], buf.at[pl.ds(0, 15)], sem).wait()

    def wait_all(buf, sem):
        pltpu.make_async_copy(buf, buf, sem).wait()

    sub = lax.broadcasted_iota(jnp.int32, (8, 128), 0)
    lane = lax.broadcasted_iota(jnp.int32, (8, 128), 1)

    def tile(read):
        t = jnp.full((8, 128), read(0))
        for r in range(1, 8):
            t = jnp.where(sub == r, read(r), t)
        return t

    zc = tile(lambda r: zc_s[r])
    mc = tile(lambda r: mc_s[r])
    mct[...] = mc
    own = lambda ref: tile(lambda r: ref[8 * g + r])
    halo = lambda ref: jnp.where(sub == 0, ref[(8 * g + 8) % 64], ref[(8 * g + 63) % 64])
    keep_o = own(msk_s) > 0
    keep_h = halo(msk_s) > 0
    valid = jnp.logical_or(
        jnp.logical_and(sub >= 4, jnp.full((8, 128), g) > 0),
        jnp.logical_and(sub < 4, jnp.full((8, 128), g) < NG - 1),
    )

    loads[0].wait()
    pl.semaphore_wait(bar, 47)
    forward(0, pv)
    rcopy(mct, mcp, 6, esem.at[0], up, me)
    rcopy(mct, mcn, 6, esem.at[1], dn, me)
    loads[1].wait()
    e = jnp.zeros((8, 128), F32)
    for k in range(NL):
        uk = uv[k]
        e = jnp.where(lane == k, pltpu.roll(uk, (k + 1) % 128, 1), e)
        e = jnp.where(lane == 32 + k, pltpu.roll(uk, 32 + k, 1), e)
    eu[...] = e
    rcopy(eu, eul, 7, esem.at[2], g, east)
    rcopy(eu, eur, 7, esem.at[3], g, west)
    loads[2].wait()
    rcopy(vv.at[:, 7:8], ev.at[:, 7:8], 8, esem.at[4], up, me)
    rcopy(vv.at[:, 0:1], ev.at[:, 0:1], 9, esem.at[5], dn, me)

    def factors(cut):
        k1 = lax.broadcasted_iota(jnp.int32, (16, 8, 128), 0)
        k2 = lax.broadcasted_iota(jnp.int32, (16, 8, 128), 2)
        k = k1 + 16 * k2
        kk = jnp.minimum(k, 2048 - k).astype(F32)
        c = cut.astype(F32)[None]
        ratio = c / jnp.maximum(kk, 1.0)
        f = jnp.where(kk > c, ratio * ratio, 1.0) * (1.0 / 2048.0)
        return f.reshape(128, 128)

    fo[...] = factors(own(cut_s))
    fh[...] = factors(halo(cut_s))

    loads[3].wait()
    prev = jnp.zeros((8, 128), F32)
    for k in range(NL):
        al = a_s[k]
        below = al * sv[k]
        above = al * sv[k + 1] if k + 1 < NL else jnp.zeros((8, 128), F32)
        ip = 1.0 / (1.0 + below + above + below * prev)
        prev = -above * ip
        rat[k] = prev
        inv[k] = ip
        qq[k] = below * ip

    wait_all(mcp, esem.at[0])
    wait_all(mcn, esem.at[1])
    mch = jnp.where(sub >= 4, mcp[...], mcn[...])
    mch = jnp.where(valid, mch, 0.0)
    wait_all(eul, esem.at[2])
    wait_all(eur, esem.at[3])
    wait_all(ev.at[:, 7:8], esem.at[4])
    wait_all(ev.at[:, 0:1], esem.at[5])
    el, er = eul[...], eur[...]
    for k in range(NL):
        uk, vk = uv[k], vv[k]
        evk = jnp.where(valid, ev[k], 0.0)
        right = jnp.where(lane == 127, pltpu.roll(er, (95 - k) % 128, 1), pltpu.roll(uk, 127, 1))
        left = jnp.where(lane == 0, pltpu.roll(el, (128 - k) % 128, 1), pltpu.roll(uk, 1, 1))
        north = pltpu.roll(jnp.where(sub == 0, evk, vk), 7, 0)
        south = pltpu.roll(jnp.where(sub == 7, evk, vk), 1, 0)
        div0[k] = zc * (right - left) + mc * (north - south)

    loads[4].wait()
    loads[5].wait()
    loads[6].wait()

    def get_main(ph, d, l):
        x = xm[0, d, l]
        return x + xm[1, d, l] if ph else x

    def get_edge(ph, d, l):
        x = xe[0, d, l]
        x = x + xe[1, d, l] if ph else x
        return jnp.where(valid, x, 0.0)

    def store_spec(t, spec):
        for k1 in range(16):
            r, i = spec[k1]
            tr, ti = tw[0, k1 : k1 + 1, :], tw[1, k1 : k1 + 1, :]
            row = t * 128 + k1 * 8
            lhs[row : row + 8, 0:128] = r * tr - i * ti
            lhs[row : row + 8, 128:256] = r * ti + i * tr

    def big_dot(x):
        return jnp.dot(x, mat[...], precision=lax.Precision.HIGHEST, preferred_element_type=F32)

    def unfold(t):
        x = []
        for k1 in range(16):
            row = t * 128 + k1 * 8
            r, i = res[row : row + 8, 0:128], res[row : row + 8, 128:256]
            tr, ti = tw[0, k1 : k1 + 1, :], tw[1, k1 : k1 + 1, :]
            x.append((r * tr - i * ti, r * ti + i * tr))
        return [(b, a) for a, b in dft16(x)]

    def level_part(ph):
        wait15(xm.at[ph], fmsem.at[ph])
        wait_all(xe.at[ph, :, :, 0:2], fesem.at[ph, 0])
        wait_all(xe.at[ph, :, :, 0:2], fesem.at[ph, 1])
        for l in range(2):
            z = []
            for d in range(16):
                x, ee = get_main(ph, d, l), get_edge(ph, d, l)
                xu, xd = pltpu.roll(x, 7, 0), pltpu.roll(x, 1, 0)
                eu_, ed_ = pltpu.roll(ee, 7, 0), pltpu.roll(ee, 1, 0)
                b = jnp.where(sub == 7, eu_, xu) - jnp.where(sub == 0, ed_, xd)
                hs[l, d] = jnp.where(sub == 0, eu_ - xd, xu - ed_)
                bs[l, d] = b
                z.append((x, b))
            store_spec(l, dft16(z))
        store_spec(2, dft16([(hs[0, d], hs[1, d]) for d in range(16)]))
        spec = big_dot(lhs[...])
        for t, f in ((0, fo), (1, fo), (2, fh)):
            lhs[t * 128 : t * 128 + 128, 0:128] = spec[t * 128 : t * 128 + 128, 128:256] * f[...]
            lhs[t * 128 : t * 128 + 128, 128:256] = spec[t * 128 : t * 128 + 128, 0:128] * f[...]
        res[...] = big_dot(lhs[...])
        hh = unfold(2)
        for d in range(16):
            for l in range(2):
                hs[l, d] = -mch * jnp.where(keep_h, hh[d][l], hs[l, d])
        for l in range(2):
            y = unfold(l)
            fa = [jnp.where(keep_o, y[d][0], get_main(ph, d, l)) for d in range(16)]
            for d in range(16):
                dvd = -mc * jnp.where(keep_o, y[d][1], bs[l, d])
                hv = hs[l, d]
                north = pltpu.roll(jnp.where(sub == 0, hv, dvd), 7, 0)
                south = pltpu.roll(jnp.where(sub == 7, hv, dvd), 1, 0)
                nx, pv_ = fa[(d + 1) % 16], fa[(d + 15) % 16]
                r2 = pltpu.roll(jnp.where(lane < 2, nx, fa[d]), 126, 1)
                l2 = pltpu.roll(jnp.where(lane >= 126, pv_, fa[d]), 2, 1)
                dd = (r2 - fa[d]) - (fa[d] - l2)
                dsend[ph, d, l] = mc * (north - south) - zc * zc * dd
                if ph == SUBSTEPS - 1:
                    dv[d, l] = dvd
                    r1 = pltpu.roll(jnp.where(lane < 1, nx, fa[d]), 127, 1)
                    l1 = pltpu.roll(jnp.where(lane >= 127, pv_, fa[d]), 1, 1)
                    du[d, l] = -zc * (r1 - l1)

    def backward(src, dst, si, sem):
        for off in OFFS:
            d = target(off)
            if off != (0, 0):
                rcopy(src.at[d], dst.at[pl.ds(2 * me, 2)], si, sem, g, d)
        dst[pl.ds(2 * me, 2)] = src[pl.ds(me, 1)][0]

    def wait30(buf, sem):
        pltpu.make_async_copy(buf.at[pl.ds(0, 30)], buf.at[pl.ds(0, 30)], sem).wait()

    def column(ph, pin, win, pout, wout):
        ps = [pin[k] - sv[k] * (div0[k] + back[ph, k]) for k in range(NL)]
        vals = []
        pval = jnp.zeros((8, 128), F32)
        for k in range(NL):
            al = a_s[k]
            if k + 1 < NL:
                rhs = win[k] - al * (ps[k + 1] - ps[k])
            else:
                rhs = win[k] + al * ps[k]
            pval = rhs * inv[k] + qq[k] * pval
            vals.append(pval)
        wk = vals[-1]
        for k in range(NL - 1, -1, -1):
            wout[k] = wk
            if k:
                wlow = vals[k - 1] - rat[k - 1] * wk
                pout[k] = ps[k] - sv[k] * (wk - wlow)
                wk = wlow
            else:
                pout[k] = ps[k] - sv[k] * wk

    outs = []

    def put(src, dst, i):
        c = pltpu.make_async_copy(src, dst, outsem.at[i])
        c.start()
        outs.append(c)

    level_part(0)
    backward(dsend.at[0], back.at[0], 10, bksem.at[0])
    wait30(back.at[0], bksem.at[0])
    column(0, pv, wv, p1, w1)
    forward(1, p1)
    level_part(1)
    backward(dsend.at[1], back.at[1], 11, bksem.at[1])
    backward(du, ru, 12, bksem.at[2])
    backward(dv, rv, 13, bksem.at[3])
    wait30(back.at[1], bksem.at[1])
    column(1, p1, w1, p2, w2)
    put(w2, wo_h, 0)
    put(p2, po_h, 1)
    wait30(ru, bksem.at[2])
    for k in range(NL):
        ru[k] = ru[k] + uv[k]
    put(ru, uo_h, 2)
    wait30(rv, bksem.at[3])
    for k in range(NL):
        rv[k] = rv[k] + vv[k]
    put(rv, vo_h, 3)

    for ph in range(SUBSTEPS):
        wait15(xm.at[ph], sendsem.at[3 * ph])
        wait_all(xe.at[ph, :, :, 0:2], sendsem.at[3 * ph + 1])
        wait_all(xe.at[ph, :, :, 0:2], sendsem.at[3 * ph + 2])
    wait_all(back.at[0, 0:2], sendsem.at[6])
    wait_all(back.at[0, 0:2], sendsem.at[7])
    wait_all(ev.at[:, 0:1], sendsem.at[8])
    wait_all(ev.at[:, 0:1], sendsem.at[9])
    for i in range(10, 14):
        wait30(ru, sendsem.at[i])
    for c in outs:
        c.wait()


def solution(mesh):
    mat_np, tw_np = tables()
    field = jax.ShapeDtypeStruct((NL, 8, 128), F32)
    smem = pl.BlockSpec(memory_space=pltpu.SMEM)
    hbm = pl.BlockSpec(memory_space=pltpu.HBM)
    blk = pltpu.VMEM((NL, 8, 128), F32)
    pair = pltpu.VMEM((2, 16, 8, 128), F32)
    quad = pltpu.VMEM((2, 16, 2, 8, 128), F32)
    line = pltpu.VMEM((8, 128), F32)
    rows = pltpu.VMEM((384, 256), F32)
    dma = pltpu.SemaphoreType.DMA
    scratch = [
        blk, blk, blk, blk, blk, pltpu.VMEM((256, 256), F32), pltpu.VMEM((2, 16, 128), F32),
        blk, blk, blk, blk, quad, quad, pair, pair, rows, rows, quad, pltpu.VMEM((2, NL, 8, 128), F32),
        pltpu.VMEM((16, 2, 8, 128), F32), pltpu.VMEM((16, 2, 8, 128), F32), blk, blk,
        blk, blk, blk, blk, line, line, line, blk, line, line, line,
        pltpu.VMEM((128, 128), F32), pltpu.VMEM((128, 128), F32),
        dma((7,)), dma((4,)), dma((14,)), dma((2,)), dma((2, 2)), dma((4,)), dma((6,)),
    ]
    call = pl.pallas_call(
        kernel,
        out_shape=(field,) * 4,
        in_specs=[smem] * 5 + [hbm] * 7,
        out_specs=(hbm,) * 4,
        scratch_shapes=scratch,
        compiler_params=pltpu.CompilerParams(collective_id=0, has_side_effects=True),
    )

    def body(u, v, w, p, zc, mc, a, s, cutoff, mask):
        return call(zc, mc, a, cutoff, mask, u, v, w, p, s, jnp.asarray(mat_np), jnp.asarray(tw_np))

    f = P(None, "lat", "lon")
    return jax.shard_map(
        body,
        mesh=mesh,
        in_specs=(f, f, f, f, P("lat"), P("lat"), P(None), f, P(None), P(None)),
        out_specs=(f,) * 4,
        check_vma=False,
    )
```

time: 479 us -> 41.7 us (0.09); the launches traced: 473 us -> 41.6 us
  matrix products: 313 us -> 0 us
  other arithmetic: 47.7 us -> 0 us
  blocking collectives: 39 us -> 0 us
  starting transfers between devices: 39 us -> 0 us
  Pallas kernels: 0 us -> 36.7 us
  waiting for transfers between devices: 25.7 us -> 0 us
    dot_general x4 -> x0, matrix products: 313 us -> none  [the longest x2 163 us: transform_band(): jnp.einsum('vetc,cj->vetj', scaled, inverse, precision=lax.Precision.HIGH...]
    div x2 -> x0, other arithmetic: 39.1 us -> none  [column_solve(): prev_value = (rhs + below * prev_value) / pivot]
    all_to_all x4 -> x0, blocking collectives: 39 us -> none  [the longest x3 27.2 us: exchange_in_order(): out = lax.all_to_all(out, axes[k], k, k, tiled=True)]
    pallas_call x0 -> x1, Pallas kernels: none -> 36.7 us  [body(): call(zc, mc, a, cutoff, mask, u, v, w, p, s, jnp.asarray(mat_np), jnp.asa...]
    ppermute x16 -> x0, starting transfers between devices: 31.6 us -> none  [the longest x8 28.6 us: padded_2(): lax.ppermute(initial, axis, [(b, a) for a, b in up])]
    all_to_all x2 -> x0, waiting for transfers between devices: 14.5 us -> none  [the longest x1 8.67 us: transform_band(): lax.all_to_all(block, LON, split_axis=1, concat_axis=3, tiled=True)]
    ppermute x16 -> x0, waiting for transfers between devices: 11.2 us -> none  [the longest x8 7.85 us: padded_2(): lax.ppermute(last, axis, up)]
    all_to_all x2 -> x0, starting transfers between devices: 7.4 us -> none  [the longest x1 4 us: transform_band(): lax.all_to_all(block, LON, split_axis=1, concat_axis=3, tiled=True)]
  transfers between devices with their start and end apart: 18 -> 0, of which waited for: 8 -> 0; matrix products, arithmetic and copies ran while one was open for 1% -> 0% of each run, Pallas kernels for 0% -> 0%
where the time goes in v1:
time: 41.7 us; the launch traced here: 41.6 us
  Pallas kernels  36.7 us (88%)
  local copies, waits for them, and re-layouts  4.16 us (10%)
  between operations  0.65 us (2%)
    pallas_call x1, Pallas kernels, body(): call(zc, mc, a, cutoff, mask, u, v, w, p, s, jnp.asarray(mat_np), jnp.asa...  36.7 us
    unnamed x10, local copies, waits for them, and re-layouts  4.16 us

profile of v1, /device:TPU:0, one launch (start us, length us, event | category | flops | bytes accessed | tf_op | source)
XLA Modules:
  0.0 41.6 jit_solution(10220746869855860729)
XLA Ops:
  0.6 36.7 %shard_map.147 = (f32[32,8,128]{2,1,0:T(8,128)}, f32[32,8,128]{2,1,0:T(8,128)}, f32[32,8,128]{2,1,0:T(8,128)}, f32[32,8,128]{2,1,0:T(8,128)}) custom-call(f32[8]{0:T(128)} %zc_s.1, f32[8]{0:T(128)} %mc_s.1, f32[32]{0:T(128)} %a_s.1, s32[64]{0:T(128)} %cut_s.1, s32[64]{0:T(128)} %msk_s.1, f32[32,8,128]{2,1,0:T(8,128)} %u_h.1, f32[32,8,128]{2,1,0:T(8,128)} %v_h.1, ...), custom_call_target="tpu_custom_call" | custom-call | tf_op jit(solution)/shard_map/pallas_call | solution.py:390
  37.4 0.0 copy-start.2
  37.4 1.6 %copy.20 = f32[32,8,128]{2,1,0:T(8,128)} copy(f32[32,8,128]{2,1,0:T(8,128)} %get-tuple-element.8) | data formatting | bytes 262144
  39.0 0.0 copy-done.2
  39.0 0.0 copy-start.1
  39.0 0.7 %copy.21 = f32[32,8,128]{2,1,0:T(8,128)} copy(f32[32,8,128]{2,1,0:T(8,128)S(1)} %copy-done.2) | data formatting | bytes 262144
  39.7 0.3 copy-done.1
  39.9 0.0 copy-start
  39.9 0.7 %copy.22 = f32[32,8,128]{2,1,0:T(8,128)} copy(f32[32,8,128]{2,1,0:T(8,128)S(1)} %copy-done.1) | data formatting | bytes 262144
  40.6 0.3 copy-done
  40.9 0.7 %copy.23 = f32[32,8,128]{2,1,0:T(8,128)} copy(f32[32,8,128]{2,1,0:T(8,128)S(1)} %copy-done) | data formatting | bytes 262144
Async XLA Ops:
  37.4 1.6 %copy-start.2 = (f32[32,8,128]{2,1,0:T(8,128)S(1)}, f32[32,8,128]{2,1,0:T(8,128)}, u32[]{:S(2)}) copy-start(f32[32,8,128]{2,1,0:T(8,128)} %get-tuple-element.9) | copy-start | bytes 393220
  39.0 1.0 %copy-start.1 = (f32[32,8,128]{2,1,0:T(8,128)S(1)}, f32[32,8,128]{2,1,0:T(8,128)}, u32[]{:S(2)}) copy-start(f32[32,8,128]{2,1,0:T(8,128)} %get-tuple-element.10) | copy-start | bytes 393220
  39.9 1.0 %copy-start = (f32[32,8,128]{2,1,0:T(8,128)S(1)}, f32[32,8,128]{2,1,0:T(8,128)}, u32[]{:S(2)}) copy-start(f32[32,8,128]{2,1,0:T(8,128)} %get-tuple-element.11) | copy-start | bytes 393220

commit v2 on v1

v2 whole, which is shorter than its diff:
```python
import math

import jax
import jax.numpy as jnp
import numpy as np
from jax import lax
from jax.experimental import pallas as pl
from jax.experimental.pallas import tpu as pltpu
from jax.sharding import PartitionSpec as P

SUBSTEPS = 2
F32 = jnp.float32
NG = 8
ND = 16
NL = 32
MESH = pl.DeviceIdType.MESH


def tables():
    lane = np.arange(128)
    ang = 2.0 * np.pi * ((lane[:, None] * lane[None, :]) % 128) / 128.0
    c, s = np.cos(ang), np.sin(ang)
    mat = np.block([[c, -s], [s, c]])
    high = mat.astype(np.float32).astype(jnp.bfloat16)
    low = (mat - high.astype(np.float64)).astype(np.float32).astype(jnp.bfloat16)
    mat = np.stack([high, low])
    tang = 2.0 * np.pi * (np.arange(16)[:, None] * lane[None, :]) / 2048.0
    tw = np.stack([np.cos(tang), -np.sin(tang)]).astype(np.float32)
    return mat, tw


def dft4(x):
    (ar, ai), (br, bi), (cr, ci), (dr, di) = x
    sr, si = ar + cr, ai + ci
    tr, ti = ar - cr, ai - ci
    ur, ui = br + dr, bi + di
    vr, vi = br - dr, bi - di
    return [(sr + ur, si + ui), (tr + vi, ti - vr), (sr - ur, si - ui), (tr - vi, ti + vr)]


def dft16(x):
    cols = []
    for n2 in range(4):
        y = dft4([x[4 * n1 + n2] for n1 in range(4)])
        out = []
        for k1 in range(4):
            e = (n2 * k1) % 16
            yr, yi = y[k1]
            if e == 0:
                out.append((yr, yi))
            elif e == 4:
                out.append((yi, -yr))
            else:
                c, s = math.cos(2 * math.pi * e / 16), math.sin(2 * math.pi * e / 16)
                out.append((yr * c + yi * s, yi * c - yr * s))
        cols.append(out)
    res = [None] * 16
    for k1 in range(4):
        z = dft4([cols[n2][k1] for n2 in range(4)])
        for k2 in range(4):
            res[k1 + 4 * k2] = z[k2]
    return res


def hops(off):
    return sum(min(o, 4 - o) for o in off)


OFFS = sorted([(a, b) for a in range(4) for b in range(4)], key=lambda o: -hops(o))


def kernel(
    zc_h, mc_h, a_h, cut_h, msk_h, u_h, v_h, w_h, p_h, s_h, mat_h, tw_h,
    uo, vo, w2, p2,
    uv, vv, wv, pv, sv, mat, tw, p1, w1, xm, xe, bs, hs, lhs, res, dsend, back,
    du, dv, ru, rv, rat, inv, qq, div0, eu, eul, eur, ev, mct, mcp, mcn, fo, fh,
    zc_s, mc_s, a_s, cut_s, msk_s,
    ldsem, smsem, sendsem, fmsem, fesem, bksem, esem,
):
    me = lax.axis_index("lon")
    g = lax.axis_index("lat")
    up = (g + 1) % NG
    dn = (g + NG - 1) % NG
    my, mx = me // 4, me % 4
    east = (me + 1) % ND
    west = (me + ND - 1) % ND

    loads = [
        pltpu.make_async_copy(a, b, ldsem.at[i])
        for i, (a, b) in enumerate(
            [(p_h, pv), (u_h, uv), (v_h, vv), (s_h, sv), (w_h, wv), (tw_h, tw), (mat_h, mat)]
        )
    ]
    small = [
        pltpu.make_async_copy(a, b, smsem.at[i])
        for i, (a, b) in enumerate(
            [(zc_h, zc_s), (mc_h, mc_s), (a_h, a_s), (cut_h, cut_s), (msk_h, msk_s)]
        )
    ]
    bar = pltpu.get_barrier_semaphore()

    def target(off):
        return ((my + off[0]) % 4) * 4 + (mx + off[1]) % 4

    for off in OFFS:
        d = target(off)
        pl.semaphore_signal(bar, inc=1, device_id={"lat": up, "lon": d}, device_id_type=MESH)
        pl.semaphore_signal(bar, inc=1, device_id={"lat": dn, "lon": d}, device_id_type=MESH)
        if off != (0, 0):
            pl.semaphore_signal(bar, inc=1, device_id={"lat": g, "lon": d}, device_id_type=MESH)

    for c in loads[:1] + small + loads[1:]:
        c.start()

    def rcopy(src, dst, si, sem, gg, d):
        c = pltpu.make_async_remote_copy(
            src_ref=src, dst_ref=dst, send_sem=sendsem.at[si], recv_sem=sem,
            device_id={"lat": gg, "lon": d}, device_id_type=MESH,
        )
        c.start()

    def forward(ph, src):
        for off in OFFS:
            d = target(off)
            if off != (0, 0):
                rcopy(src.at[pl.ds(2 * d, 2)], xm.at[ph, me], 3 * ph, fmsem.at[ph], g, d)
            rcopy(src.at[pl.ds(2 * d, 2), 6:8], xe.at[ph, me, :, 6:8], 3 * ph + 1, fesem.at[ph, 0], up, d)
            rcopy(src.at[pl.ds(2 * d, 2), 0:2], xe.at[ph, me, :, 0:2], 3 * ph + 2, fesem.at[ph, 1], dn, d)
        xm[ph, pl.ds(me, 1)] = src[pl.ds(2 * me, 2)][None]

    def wait15(buf, sem):
        pltpu.make_async_copy(buf.at[pl.ds(0, 15)], buf.at[pl.ds(0, 15)], sem).wait()

    def wait_all(buf, sem):
        pltpu.make_async_copy(buf, buf, sem).wait()

    sub = lax.broadcasted_iota(jnp.int32, (8, 128), 0)
    lane = lax.broadcasted_iota(jnp.int32, (8, 128), 1)

    def tile(read):
        t = jnp.full((8, 128), read(0))
        for r in range(1, 8):
            t = jnp.where(sub == r, read(r), t)
        return t

    valid = jnp.logical_or(
        jnp.logical_and(sub >= 4, jnp.full((8, 128), g) > 0),
        jnp.logical_and(sub < 4, jnp.full((8, 128), g) < NG - 1),
    )

    with jax.named_scope("entry"):
        loads[0].wait()
        pl.semaphore_wait(bar, 47)
    with jax.named_scope("fwd0"):
        forward(0, pv)
        for c in small:
            c.wait()
        zc = tile(lambda r: zc_s[r])
        mc = tile(lambda r: mc_s[r])
        mct[...] = mc
        own = lambda ref: tile(lambda r: ref[8 * g + r])
        halo = lambda ref: jnp.where(sub == 0, ref[(8 * g + 8) % 64], ref[(8 * g + 63) % 64])
        keep_o = own(msk_s) > 0
        keep_h = halo(msk_s) > 0
        rcopy(mct, mcp, 6, esem.at[0], up, me)
        rcopy(mct, mcn, 6, esem.at[1], dn, me)
    with jax.named_scope("home"):
        loads[1].wait()
        e = jnp.zeros((8, 128), F32)
        for k in range(NL):
            uk = uv[k]
            e = jnp.where(lane == k, pltpu.roll(uk, (k + 1) % 128, 1), e)
            e = jnp.where(lane == 32 + k, pltpu.roll(uk, 32 + k, 1), e)
        eu[...] = e
        rcopy(eu, eul, 7, esem.at[2], g, east)
        rcopy(eu, eur, 7, esem.at[3], g, west)
        loads[2].wait()
        rcopy(vv.at[:, 7:8], ev.at[:, 7:8], 8, esem.at[4], up, me)
        rcopy(vv.at[:, 0:1], ev.at[:, 0:1], 9, esem.at[5], dn, me)

        def factors(cut):
            k1 = lax.broadcasted_iota(jnp.int32, (16, 8, 128), 0)
            k2 = lax.broadcasted_iota(jnp.int32, (16, 8, 128), 2)
            k = k1 + 16 * k2
            kk = jnp.minimum(k, 2048 - k).astype(F32)
            c = cut.astype(F32)[None]
            ratio = c / jnp.maximum(kk, 1.0)
            f = jnp.where(kk > c, ratio * ratio, 1.0) * (1.0 / 2048.0)
            return f.reshape(128, 128)

        fo[...] = factors(own(cut_s))
        fh[...] = factors(halo(cut_s))

        loads[3].wait()
        prev = jnp.zeros((8, 128), F32)
        for k in range(NL):
            al = a_s[k]
            below = al * sv[k]
            above = al * sv[k + 1] if k + 1 < NL else jnp.zeros((8, 128), F32)
            ip = 1.0 / (1.0 + below + above + below * prev)
            prev = -above * ip
            rat[k] = prev
            inv[k] = ip
            qq[k] = below * ip

        wait_all(mcp, esem.at[0])
        wait_all(mcn, esem.at[1])
        mch = jnp.where(sub >= 4, mcp[...], mcn[...])
        mch = jnp.where(valid, mch, 0.0)
        wait_all(eul, esem.at[2])
        wait_all(eur, esem.at[3])
        wait_all(ev.at[:, 7:8], esem.at[4])
        wait_all(ev.at[:, 0:1], esem.at[5])
        el, er = eul[...], eur[...]
        for k in range(NL):
            uk, vk = uv[k], vv[k]
            evk = jnp.where(valid, ev[k], 0.0)
            right = jnp.where(lane == 127, pltpu.roll(er, (95 - k) % 128, 1), pltpu.roll(uk, 127, 1))
            left = jnp.where(lane == 0, pltpu.roll(el, (128 - k) % 128, 1), pltpu.roll(uk, 1, 1))
            north = pltpu.roll(jnp.where(sub == 0, evk, vk), 7, 0)
            south = pltpu.roll(jnp.where(sub == 7, evk, vk), 1, 0)
            div0[k] = zc * (right - left) + mc * (north - south)
    loads[4].wait()
    loads[5].wait()
    loads[6].wait()

    def get_main(ph, d, l):
        x = xm[0, d, l]
        return x + xm[1, d, l] if ph else x

    def get_edge(ph, d, l):
        x = xe[0, d, l]
        x = x + xe[1, d, l] if ph else x
        return jnp.where(valid, x, 0.0)

    def store_spec(t, spec):
        for k1 in range(16):
            r, i = spec[k1]
            tr, ti = tw[0, k1 : k1 + 1, :], tw[1, k1 : k1 + 1, :]
            row = t * 128 + k1 * 8
            lhs[row : row + 8, 0:128] = r * tr - i * ti
            lhs[row : row + 8, 128:256] = r * ti + i * tr

    def big_dot(x):
        high = x.astype(jnp.bfloat16)
        low = (x - high.astype(F32)).astype(jnp.bfloat16)
        one = lambda a, b: jnp.dot(a, b, preferred_element_type=F32)
        return one(high, mat[0]) + one(low, mat[0]) + one(high, mat[1])

    def unfold(t):
        x = []
        for k1 in range(16):
            row = t * 128 + k1 * 8
            r, i = res[row : row + 8, 0:128], res[row : row + 8, 128:256]
            tr, ti = tw[0, k1 : k1 + 1, :], tw[1, k1 : k1 + 1, :]
            x.append((r * tr - i * ti, r * ti + i * tr))
        return [(b, a) for a, b in dft16(x)]

    def level_part(ph):
        with jax.named_scope("waitf%d" % ph):
            wait15(xm.at[ph], fmsem.at[ph])
            wait_all(xe.at[ph, :, :, 0:2], fesem.at[ph, 0])
            wait_all(xe.at[ph, :, :, 0:2], fesem.at[ph, 1])
        with jax.named_scope("fold%d" % ph):
            for l in range(2):
                z = []
                for d in range(16):
                    x, ee = get_main(ph, d, l), get_edge(ph, d, l)
                    xu, xd = pltpu.roll(x, 7, 0), pltpu.roll(x, 1, 0)
                    eu_, ed_ = pltpu.roll(ee, 7, 0), pltpu.roll(ee, 1, 0)
                    b = jnp.where(sub == 7, eu_, xu) - jnp.where(sub == 0, ed_, xd)
                    hs[l, d] = jnp.where(sub == 0, eu_ - xd, xu - ed_)
                    bs[l, d] = b
                    z.append((x, b))
                store_spec(l, dft16(z))
            store_spec(2, dft16([(hs[0, d], hs[1, d]) for d in range(16)]))
        with jax.named_scope("dots%d" % ph):
            spec = big_dot(lhs[...])
            for t, f in ((0, fo), (1, fo), (2, fh)):
                lhs[t * 128 : t * 128 + 128, 0:128] = spec[t * 128 : t * 128 + 128, 128:256] * f[...]
                lhs[t * 128 : t * 128 + 128, 128:256] = spec[t * 128 : t * 128 + 128, 0:128] * f[...]
            res[...] = big_dot(lhs[...])
        with jax.named_scope("unfold%d" % ph):
            hh = unfold(2)
            for d in range(16):
                for l in range(2):
                    hs[l, d] = -mch * jnp.where(keep_h, hh[d][l], hs[l, d])
            for l in range(2):
                y = unfold(l)
                fa = [jnp.where(keep_o, y[d][0], get_main(ph, d, l)) for d in range(16)]
                for d in range(16):
                    dvd = -mc * jnp.where(keep_o, y[d][1], bs[l, d])
                    hv = hs[l, d]
                    north = pltpu.roll(jnp.where(sub == 0, hv, dvd), 7, 0)
                    south = pltpu.roll(jnp.where(sub == 7, hv, dvd), 1, 0)
                    nx, pv_ = fa[(d + 1) % 16], fa[(d + 15) % 16]
                    r2 = pltpu.roll(jnp.where(lane < 2, nx, fa[d]), 126, 1)
                    l2 = pltpu.roll(jnp.where(lane >= 126, pv_, fa[d]), 2, 1)
                    dd = (r2 - fa[d]) - (fa[d] - l2)
                    dsend[ph, d, l] = mc * (north - south) - zc * zc * dd
                    if ph == SUBSTEPS - 1:
                        dv[d, l] = dvd
                        r1 = pltpu.roll(jnp.where(lane < 1, nx, fa[d]), 127, 1)
                        l1 = pltpu.roll(jnp.where(lane >= 127, pv_, fa[d]), 1, 1)
                        du[d, l] = -zc * (r1 - l1)
    def backward(src, dst, si, sem):
        for off in OFFS:
            d = target(off)
            if off != (0, 0):
                rcopy(src.at[d], dst.at[pl.ds(2 * me, 2)], si, sem, g, d)
        dst[pl.ds(2 * me, 2)] = src[pl.ds(me, 1)][0]

    def wait30(buf, sem):
        pltpu.make_async_copy(buf.at[pl.ds(0, 30)], buf.at[pl.ds(0, 30)], sem).wait()

    def column(ph, pin, win, pout, wout):
        ps = [pin[k] - sv[k] * (div0[k] + back[ph, k]) for k in range(NL)]
        vals = []
        pval = jnp.zeros((8, 128), F32)
        for k in range(NL):
            al = a_s[k]
            if k + 1 < NL:
                rhs = win[k] - al * (ps[k + 1] - ps[k])
            else:
                rhs = win[k] + al * ps[k]
            pval = rhs * inv[k] + qq[k] * pval
            vals.append(pval)
        wk = vals[-1]
        for k in range(NL - 1, -1, -1):
            wout[k] = wk
            if k:
                wlow = vals[k - 1] - rat[k - 1] * wk
                pout[k] = ps[k] - sv[k] * (wk - wlow)
                wk = wlow
            else:
                pout[k] = ps[k] - sv[k] * wk

    level_part(0)
    with jax.named_scope("bk0"):
        backward(dsend.at[0], back.at[0], 10, bksem.at[0])
    with jax.named_scope("waitb0"):
        wait30(back.at[0], bksem.at[0])
    with jax.named_scope("col0"):
        column(0, pv, wv, p1, w1)
    with jax.named_scope("fwd1"):
        forward(1, p1)
    level_part(1)
    with jax.named_scope("bk1"):
        backward(dsend.at[1], back.at[1], 11, bksem.at[1])
        backward(du, ru, 12, bksem.at[2])
        backward(dv, rv, 13, bksem.at[3])
    with jax.named_scope("waitb1"):
        wait30(back.at[1], bksem.at[1])
    with jax.named_scope("col1"):
        column(1, p1, w1, p2, w2)
    with jax.named_scope("fin"):
        wait30(ru, bksem.at[2])
        for k in range(NL):
            uo[k] = ru[k] + uv[k]
        wait30(rv, bksem.at[3])
        for k in range(NL):
            vo[k] = rv[k] + vv[k]
    with jax.named_scope("sends"):
        for ph in range(SUBSTEPS):
            wait15(xm.at[ph], sendsem.at[3 * ph])
            wait_all(xe.at[ph, :, :, 0:2], sendsem.at[3 * ph + 1])
            wait_all(xe.at[ph, :, :, 0:2], sendsem.at[3 * ph + 2])
        wait_all(back.at[0, 0:2], sendsem.at[6])
        wait_all(back.at[0, 0:2], sendsem.at[7])
        wait_all(ev.at[:, 0:1], sendsem.at[8])
        wait_all(ev.at[:, 0:1], sendsem.at[9])
        for i in range(10, 14):
            wait30(ru, sendsem.at[i])

def store(u, v, w, p, uo, vo, wo, po, sem):
    copies = [pltpu.make_async_copy(a, b, sem.at[i]) for i, (a, b) in enumerate([(u, uo), (v, vo), (w, wo), (p, po)])]
    for c in copies:
        c.start()
    for c in copies:
        c.wait()


def solution(mesh):
    mat_np, tw_np = tables()
    field = jax.ShapeDtypeStruct((NL, 8, 128), F32)
    vmem = pl.BlockSpec(memory_space=pltpu.VMEM)
    hbm = pl.BlockSpec(memory_space=pltpu.HBM)
    blk = pltpu.VMEM((NL, 8, 128), F32)
    pair = pltpu.VMEM((2, 16, 8, 128), F32)
    quad = pltpu.VMEM((2, 16, 2, 8, 128), F32)
    line = pltpu.VMEM((8, 128), F32)
    rows = pltpu.VMEM((384, 256), F32)
    dma = pltpu.SemaphoreType.DMA
    scratch = [
        blk, blk, blk, blk, blk, pltpu.VMEM((2, 256, 256), jnp.bfloat16), pltpu.VMEM((2, 16, 128), F32),
        blk, blk, quad, quad, pair, pair, rows, rows, quad, pltpu.VMEM((2, NL, 8, 128), F32),
        pltpu.VMEM((16, 2, 8, 128), F32), pltpu.VMEM((16, 2, 8, 128), F32), blk, blk,
        blk, blk, blk, blk, line, line, line, blk, line, line, line,
        pltpu.VMEM((128, 128), F32), pltpu.VMEM((128, 128), F32),
        pltpu.SMEM((8,), F32), pltpu.SMEM((8,), F32), pltpu.SMEM((NL,), F32), pltpu.SMEM((64,), jnp.int32), pltpu.SMEM((64,), jnp.int32),
        dma((7,)), dma((5,)), dma((14,)), dma((2,)), dma((2, 2)), dma((4,)), dma((6,)),
    ]
    call = pl.pallas_call(
        kernel,
        out_shape=(blk,) * 4,
        in_specs=[hbm] * 12,
        out_specs=(vmem,) * 4,
        scratch_shapes=scratch,
        compiler_params=pltpu.CompilerParams(collective_id=0, has_side_effects=True),
    )

    finish = pl.pallas_call(
        store, out_shape=(field,) * 4, in_specs=[vmem] * 4, out_specs=(hbm,) * 4, scratch_shapes=[dma((4,))]
    )

    def hold(*xs):
        return [pltpu.with_memory_space_constraint(o, pltpu.VMEM) for o in call(*xs)]

    def body(u, v, w, p, zc, mc, a, s, cutoff, mask):
        return finish(*hold(zc, mc, a, cutoff, mask, u, v, w, p, s, jnp.asarray(mat_np), jnp.asarray(tw_np)))

    f = P(None, "lat", "lon")
    return jax.shard_map(
        body,
        mesh=mesh,
        in_specs=(f, f, f, f, P("lat"), P("lat"), P(None), f, P(None), P(None)),
        out_specs=(f,) * 4,
        check_vma=False,
    )
```

time: 41.7 us -> 35.7 us (0.86)
  local copies, waits for them, and re-layouts: 4.16 us -> 0 us
  Pallas kernels: 36.7 us -> 34.9 us
    unnamed x10 -> x0, local copies, waits for them, and re-layouts: 4.16 us -> none
    pallas_call x1 -> x2, Pallas kernels: 36.7 us -> 34.9 us  [the longest x1 34.1 us: hold(): call(*xs)]
where the time goes in v2:
time: 35.7 us; the launch traced here: 35.5 us
  Pallas kernels  34.9 us (98%)
  between operations  0.64 us (2%)
    pallas_call x1, Pallas kernels, hold(): call(*xs)  34.1 us
    pallas_call x1, Pallas kernels, body(): finish(*hold(zc, mc, a, cutoff, mask, u, v, w, p, s, jnp.asarray(mat_np),...  0.82 us

profile of v2, /device:TPU:0, one launch (start us, length us, event | category | flops | bytes accessed | tf_op | source)
XLA Modules:
  0.0 35.5 jit_solution(15369558895702362047)
XLA Ops:
  0.6 34.1 %shard_map.147 = (f32[32,8,128]{2,1,0:T(8,128)S(1)}, f32[32,8,128]{2,1,0:T(8,128)S(1)}, f32[32,8,128]{2,1,0:T(8,128)S(1)}, f32[32,8,128]{2,1,0:T(8,128)S(1)}) custom-call(f32[8]{0:T(128)} %zc_h.1, f32[8]{0:T(128)} %mc_h.1, f32[32]{0:T(128)} %a_h.1, s32[64]{0:T(128)} %cut_h.1, s32[64]{0:T(128)} %msk_h.1, f32[32,8,128]{2,1,0:T(8,128)} %u_h.1, ...), custom_call_target="tpu_custom_call" | custom-call | tf_op jit(solution)/shard_map/pallas_call | solution.py:417
  34.7 0.8 %shard_map.148 = (f32[32,8,128]{2,1,0:T(8,128)}, f32[32,8,128]{2,1,0:T(8,128)}, f32[32,8,128]{2,1,0:T(8,128)}, f32[32,8,128]{2,1,0:T(8,128)}) custom-call(f32[32,8,128]{2,1,0:T(8,128)S(1)} %get-tuple-element.8.u, f32[32,8,128]{2,1,0:T(8,128)S(1)} %get-tuple-element.9.v, f32[32,8,128]{2,1,0:T(8,128)S(1)} %get-tuple-element.10.w, ...), custom_call_target="tpu_custom_call" | custom-call | tf_op jit(solution)/shard_map/pallas_call | solution.py:420

commit v3 on v2

--- a/solution.py
+++ b/solution.py
@@ -23,7 +23,7 @@
     mat = np.block([[c, -s], [s, c]])
     high = mat.astype(np.float32).astype(jnp.bfloat16)
     low = (mat - high.astype(np.float64)).astype(np.float32).astype(jnp.bfloat16)
-    mat = np.stack([high, low])
+    mat = np.concatenate([high, high, low])
     tang = 2.0 * np.pi * (np.arange(16)[:, None] * lane[None, :]) / 2048.0
     tw = np.stack([np.cos(tang), -np.sin(tang)]).astype(np.float32)
     return mat, tw
@@ -72,8 +72,8 @@
 def kernel(
     zc_h, mc_h, a_h, cut_h, msk_h, u_h, v_h, w_h, p_h, s_h, mat_h, tw_h,
     uo, vo, w2, p2,
-    uv, vv, wv, pv, sv, mat, tw, p1, w1, xm, xe, bs, hs, lhs, res, dsend, back,
-    du, dv, ru, rv, rat, inv, qq, div0, eu, eul, eur, ev, mct, mcp, mcn, fo, fh,
+    uv, vv, wv, pv, sv, mat, tw, p1, w1, xm, xe, lhs, res, dsend, back,
+    du, dv, ru, rv, rat, inv, qq, div0, eu, eul, eur, ev, mct, mcp, mcn, fo, fb, fh,
     zc_s, mc_s, a_s, cut_s, msk_s,
     ldsem, smsem, sendsem, fmsem, fesem, bksem, esem,
 ):
@@ -122,10 +122,12 @@
     def forward(ph, src):
         for off in OFFS:
             d = target(off)
+            rcopy(src.at[pl.ds(2 * d, 2), 6:8], xe.at[ph, me, :, 6:8], 3 * ph + 1, fesem.at[ph, 0], up, d)
+            rcopy(src.at[pl.ds(2 * d, 2), 0:2], xe.at[ph, me, :, 0:2], 3 * ph + 2, fesem.at[ph, 1], dn, d)
+        for off in OFFS:
+            d = target(off)
             if off != (0, 0):
                 rcopy(src.at[pl.ds(2 * d, 2)], xm.at[ph, me], 3 * ph, fmsem.at[ph], g, d)
-            rcopy(src.at[pl.ds(2 * d, 2), 6:8], xe.at[ph, me, :, 6:8], 3 * ph + 1, fesem.at[ph, 0], up, d)
-            rcopy(src.at[pl.ds(2 * d, 2), 0:2], xe.at[ph, me, :, 0:2], 3 * ph + 2, fesem.at[ph, 1], dn, d)
         xm[ph, pl.ds(me, 1)] = src[pl.ds(2 * me, 2)][None]
 
     def wait15(buf, sem):
@@ -160,8 +162,6 @@
         mct[...] = mc
         own = lambda ref: tile(lambda r: ref[8 * g + r])
         halo = lambda ref: jnp.where(sub == 0, ref[(8 * g + 8) % 64], ref[(8 * g + 63) % 64])
-        keep_o = own(msk_s) > 0
-        keep_h = halo(msk_s) > 0
         rcopy(mct, mcp, 6, esem.at[0], up, me)
         rcopy(mct, mcn, 6, esem.at[1], dn, me)
     with jax.named_scope("home"):
@@ -178,18 +178,18 @@
         rcopy(vv.at[:, 7:8], ev.at[:, 7:8], 8, esem.at[4], up, me)
         rcopy(vv.at[:, 0:1], ev.at[:, 0:1], 9, esem.at[5], dn, me)
 
-        def factors(cut):
+        def factors(cut, mask):
             k1 = lax.broadcasted_iota(jnp.int32, (16, 8, 128), 0)
             k2 = lax.broadcasted_iota(jnp.int32, (16, 8, 128), 2)
             k = k1 + 16 * k2
             kk = jnp.minimum(k, 2048 - k).astype(F32)
             c = cut.astype(F32)[None]
             ratio = c / jnp.maximum(kk, 1.0)
-            f = jnp.where(kk > c, ratio * ratio, 1.0) * (1.0 / 2048.0)
-            return f.reshape(128, 128)
-
-        fo[...] = factors(own(cut_s))
-        fh[...] = factors(halo(cut_s))
+            damped = jnp.logical_and(kk > c, mask[None] > 0)
+            return jnp.where(damped, ratio * ratio, 1.0) * (1.0 / 2048.0)
+
+        fo[...] = factors(own(cut_s), own(msk_s)).reshape(128, 128)
+        fb[...] = (-mc[None] * factors(own(cut_s), own(msk_s))).reshape(128, 128)
 
         loads[3].wait()
         prev = jnp.zeros((8, 128), F32)
@@ -207,6 +207,7 @@
         wait_all(mcn, esem.at[1])
         mch = jnp.where(sub >= 4, mcp[...], mcn[...])
         mch = jnp.where(valid, mch, 0.0)
+        fh[...] = (-mch[None] * factors(halo(cut_s), halo(msk_s))).reshape(128, 128)
         wait_all(eul, esem.at[2])
         wait_all(eur, esem.at[3])
         wait_all(ev.at[:, 7:8], esem.at[4])
@@ -245,7 +246,7 @@
         high = x.astype(jnp.bfloat16)
         low = (x - high.astype(F32)).astype(jnp.bfloat16)
         one = lambda a, b: jnp.dot(a, b, preferred_element_type=F32)
-        return one(high, mat[0]) + one(low, mat[0]) + one(high, mat[1])
+        return one(jnp.concatenate([high, low, high], axis=1), mat[...])
 
     def unfold(t):
         x = []
@@ -256,53 +257,6 @@
             x.append((r * tr - i * ti, r * ti + i * tr))
         return [(b, a) for a, b in dft16(x)]
 
-    def level_part(ph):
-        with jax.named_scope("waitf%d" % ph):
-            wait15(xm.at[ph], fmsem.at[ph])
-            wait_all(xe.at[ph, :, :, 0:2], fesem.at[ph, 0])
-            wait_all(xe.at[ph, :, :, 0:2], fesem.at[ph, 1])
-        with jax.named_scope("fold%d" % ph):
-            for l in range(2):
-                z = []
-                for d in range(16):
-                    x, ee = get_main(ph, d, l), get_edge(ph, d, l)
-                    xu, xd = pltpu.roll(x, 7, 0), pltpu.roll(x, 1, 0)
-                    eu_, ed_ = pltpu.roll(ee, 7, 0), pltpu.roll(ee, 1, 0)
-                    b = jnp.where(sub == 7, eu_, xu) - jnp.where(sub == 0, ed_, xd)
-                    hs[l, d] = jnp.where(sub == 0, eu_ - xd, xu - ed_)
-                    bs[l, d] = b
-                    z.append((x, b))
-                store_spec(l, dft16(z))
-            store_spec(2, dft16([(hs[0, d], hs[1, d]) for d in range(16)]))
-        with jax.named_scope("dots%d" % ph):
-            spec = big_dot(lhs[...])
-            for t, f in ((0, fo), (1, fo), (2, fh)):
-                lhs[t * 128 : t * 128 + 128, 0:128] = spec[t * 128 : t * 128 + 128, 128:256] * f[...]
-                lhs[t * 128 : t * 128 + 128, 128:256] = spec[t * 128 : t * 128 + 128, 0:128] * f[...]
-            res[...] = big_dot(lhs[...])
-        with jax.named_scope("unfold%d" % ph):
-            hh = unfold(2)
-            for d in range(16):
-                for l in range(2):
-                    hs[l, d] = -mch * jnp.where(keep_h, hh[d][l], hs[l, d])
-            for l in range(2):
-                y = unfold(l)
-                fa = [jnp.where(keep_o, y[d][0], get_main(ph, d, l)) for d in range(16)]
-                for d in range(16):
-                    dvd = -mc * jnp.where(keep_o, y[d][1], bs[l, d])
-                    hv = hs[l, d]
-                    north = pltpu.roll(jnp.where(sub == 0, hv, dvd), 7, 0)
-                    south = pltpu.roll(jnp.where(sub == 7, hv, dvd), 1, 0)
-                    nx, pv_ = fa[(d + 1) % 16], fa[(d + 15) % 16]
-                    r2 = pltpu.roll(jnp.where(lane < 2, nx, fa[d]), 126, 1)
-                    l2 = pltpu.roll(jnp.where(lane >= 126, pv_, fa[d]), 2, 1)
-                    dd = (r2 - fa[d]) - (fa[d] - l2)
-                    dsend[ph, d, l] = mc * (north - south) - zc * zc * dd
-                    if ph == SUBSTEPS - 1:
-                        dv[d, l] = dvd
-                        r1 = pltpu.roll(jnp.where(lane < 1, nx, fa[d]), 127, 1)
-                        l1 = pltpu.roll(jnp.where(lane >= 127, pv_, fa[d]), 1, 1)
-                        du[d, l] = -zc * (r1 - l1)
     def backward(src, dst, si, sem):
         for off in OFFS:
             d = target(off)
@@ -312,6 +266,56 @@
 
     def wait30(buf, sem):
         pltpu.make_async_copy(buf.at[pl.ds(0, 30)], buf.at[pl.ds(0, 30)], sem).wait()
+
+    def filtered(t, spec, f):
+        turned = jnp.concatenate([spec[:, 128:256] * f[...], spec[:, 0:128] * f[...]], axis=1)
+        res[t * 128 : t * 128 + 128, :] = big_dot(turned)
+        return unfold(t)
+
+    def level_part(ph):
+        with jax.named_scope("waitm%d" % ph):
+            wait15(xm.at[ph], fmsem.at[ph])
+        with jax.named_scope("main%d" % ph):
+            store_spec(0, dft16([(get_main(ph, d, 0), get_main(ph, d, 1)) for d in range(16)]))
+            spec = big_dot(lhs[0:128, :])
+            own_spec = spec.reshape(16, 8, 256)
+            fa = filtered(0, spec, fo)
+            for d in range(16):
+                for l in range(2):
+                    x, nx, pv_ = fa[d][l], fa[(d + 1) % 16][l], fa[(d + 15) % 16][l]
+                    r2 = pltpu.roll(jnp.where(lane < 2, nx, x), 126, 1)
+                    l2 = pltpu.roll(jnp.where(lane >= 126, pv_, x), 2, 1)
+                    dsend[ph, d, l] = -zc * zc * ((r2 - x) - (x - l2))
+                    if ph == SUBSTEPS - 1:
+                        r1 = pltpu.roll(jnp.where(lane < 1, nx, x), 127, 1)
+                        l1 = pltpu.roll(jnp.where(lane >= 127, pv_, x), 1, 1)
+                        du[d, l] = -zc * (r1 - l1)
+            if ph == SUBSTEPS - 1:
+                backward(du, ru, 12, bksem.at[2])
+        with jax.named_scope("waite%d" % ph):
+            wait_all(xe.at[ph, :, :, 0:2], fesem.at[ph, 0])
+            wait_all(xe.at[ph, :, :, 0:2], fesem.at[ph, 1])
+        with jax.named_scope("edge%d" % ph):
+            store_spec(1, dft16([(get_edge(ph, d, 0), get_edge(ph, d, 1)) for d in range(16)]))
+            edge_spec = big_dot(lhs[128:256, :]).reshape(16, 8, 256)
+            wide = lax.broadcasted_iota(jnp.int32, (8, 256), 0)
+            bt, ht = [], []
+            for k1 in range(16):
+                o, e = own_spec[k1], edge_spec[k1]
+                ou, od = pltpu.roll(o, 7, 0), pltpu.roll(o, 1, 0)
+                eu_, ed_ = pltpu.roll(e, 7, 0), pltpu.roll(e, 1, 0)
+                bt.append(jnp.where(wide == 7, eu_, ou) - jnp.where(wide == 0, ed_, od))
+                ht.append(jnp.where(wide == 0, eu_ - od, ou - ed_))
+            hv = filtered(2, jnp.concatenate(ht, axis=0), fh)
+            dy = filtered(1, jnp.concatenate(bt, axis=0), fb)
+            for d in range(16):
+                for l in range(2):
+                    x, e = dy[d][l], hv[d][l]
+                    north = pltpu.roll(jnp.where(sub == 0, e, x), 7, 0)
+                    south = pltpu.roll(jnp.where(sub == 7, e, x), 1, 0)
+                    dsend[ph, d, l] = dsend[ph, d, l] + mc * (north - south)
+                    if ph == SUBSTEPS - 1:
+                        dv[d, l] = x
 
     def column(ph, pin, win, pout, wout):
         ps = [pin[k] - sv[k] * (div0[k] + back[ph, k]) for k in range(NL)]
@@ -347,7 +351,6 @@
     level_part(1)
     with jax.named_scope("bk1"):
         backward(dsend.at[1], back.at[1], 11, bksem.at[1])
-        backward(du, ru, 12, bksem.at[2])
         backward(dv, rv, 13, bksem.at[3])
     with jax.named_scope("waitb1"):
         wait30(back.at[1], bksem.at[1])
@@ -386,17 +389,16 @@
     vmem = pl.BlockSpec(memory_space=pltpu.VMEM)
     hbm = pl.BlockSpec(memory_space=pltpu.HBM)
     blk = pltpu.VMEM((NL, 8, 128), F32)
-    pair = pltpu.VMEM((2, 16, 8, 128), F32)
     quad = pltpu.VMEM((2, 16, 2, 8, 128), F32)
     line = pltpu.VMEM((8, 128), F32)
     rows = pltpu.VMEM((384, 256), F32)
     dma = pltpu.SemaphoreType.DMA
     scratch = [
-        blk, blk, blk, blk, blk, pltpu.VMEM((2, 256, 256), jnp.bfloat16), pltpu.VMEM((2, 16, 128), F32),
-        blk, blk, quad, quad, pair, pair, rows, rows, quad, pltpu.VMEM((2, NL, 8, 128), F32),
+        blk, blk, blk, blk, blk, pltpu.VMEM((768, 256), jnp.bfloat16), pltpu.VMEM((2, 16, 128), F32),
+        blk, blk, quad, quad, pltpu.VMEM((256, 256), F32), rows, quad, pltpu.VMEM((2, NL, 8, 128), F32),
         pltpu.VMEM((16, 2, 8, 128), F32), pltpu.VMEM((16, 2, 8, 128), F32), blk, blk,
         blk, blk, blk, blk, line, line, line, blk, line, line, line,
-        pltpu.VMEM((128, 128), F32), pltpu.VMEM((128, 128), F32),
+        pltpu.VMEM((128, 128), F32), pltpu.VMEM((128, 128), F32), pltpu.VMEM((128, 128), F32),
         pltpu.SMEM((8,), F32), pltpu.SMEM((8,), F32), pltpu.SMEM((NL,), F32), pltpu.SMEM((64,), jnp.int32), pltpu.SMEM((64,), jnp.int32),
         dma((7,)), dma((5,)), dma((14,)), dma((2,)), dma((2, 2)), dma((4,)), dma((6,)),
     ]

time: 35.7 us -> 34.2 us (0.958)
  Pallas kernels: 34.9 us -> 33.4 us
    pallas_call x1, Pallas kernels: 34.1 us -> 32.6 us  [hold(): call(*xs)]
where the time goes in v3:
time: 34.2 us; the launch traced here: 34 us
  Pallas kernels  33.4 us (98%)
  between operations  0.64 us (2%)
    pallas_call x1, Pallas kernels, hold(): call(*xs)  32.6 us
    pallas_call x1, Pallas kernels, body(): finish(*hold(zc, mc, a, cutoff, mask, u, v, w, p, s, jnp.asarray(mat_np),...  0.82 us

profile of v3, /device:TPU:0, one launch (start us, length us, event | category | flops | bytes accessed | tf_op | source)
XLA Modules:
  0.0 34.0 jit_solution(1769430936676266972)
XLA Ops:
  0.6 32.6 %shard_map.147 = (f32[32,8,128]{2,1,0:T(8,128)S(1)}, f32[32,8,128]{2,1,0:T(8,128)S(1)}, f32[32,8,128]{2,1,0:T(8,128)S(1)}, f32[32,8,128]{2,1,0:T(8,128)S(1)}) custom-call(f32[8]{0:T(128)} %zc_h.1, f32[8]{0:T(128)} %mc_h.1, f32[32]{0:T(128)} %a_h.1, s32[64]{0:T(128)} %cut_h.1, s32[64]{0:T(128)} %msk_h.1, f32[32,8,128]{2,1,0:T(8,128)} %u_h.1, ...), custom_call_target="tpu_custom_call" | custom-call | tf_op jit(solution)/shard_map/pallas_call | solution.py:419
  33.2 0.8 %shard_map.148 = (f32[32,8,128]{2,1,0:T(8,128)}, f32[32,8,128]{2,1,0:T(8,128)}, f32[32,8,128]{2,1,0:T(8,128)}, f32[32,8,128]{2,1,0:T(8,128)}) custom-call(f32[32,8,128]{2,1,0:T(8,128)S(1)} %get-tuple-element.8.u, f32[32,8,128]{2,1,0:T(8,128)S(1)} %get-tuple-element.9.v, f32[32,8,128]{2,1,0:T(8,128)S(1)} %get-tuple-element.10.w, ...), custom_call_target="tpu_custom_call" | custom-call | tf_op jit(solution)/shard_map/pallas_call | solution.py:422

commit v4 on v3

--- a/solution.py
+++ b/solution.py
@@ -79,6 +79,7 @@
 ):
     me = lax.axis_index("lon")
     g = lax.axis_index("lat")
+    par = g % 2
     up = (g + 1) % NG
     dn = (g + NG - 1) % NG
     my, mx = me // 4, me % 4
@@ -152,9 +153,6 @@
 
     with jax.named_scope("entry"):
         loads[0].wait()
-        pl.semaphore_wait(bar, 47)
-    with jax.named_scope("fwd0"):
-        forward(0, pv)
         for c in small:
             c.wait()
         zc = tile(lambda r: zc_s[r])
@@ -162,8 +160,11 @@
         mct[...] = mc
         own = lambda ref: tile(lambda r: ref[8 * g + r])
         halo = lambda ref: jnp.where(sub == 0, ref[(8 * g + 8) % 64], ref[(8 * g + 63) % 64])
+        pl.semaphore_wait(bar, 47)
+    with jax.named_scope("fwd0"):
         rcopy(mct, mcp, 6, esem.at[0], up, me)
         rcopy(mct, mcn, 6, esem.at[1], dn, me)
+        forward(0, pv)
     with jax.named_scope("home"):
         loads[1].wait()
         e = jnp.zeros((8, 128), F32)
@@ -191,37 +192,11 @@
         fo[...] = factors(own(cut_s), own(msk_s)).reshape(128, 128)
         fb[...] = (-mc[None] * factors(own(cut_s), own(msk_s))).reshape(128, 128)
 
-        loads[3].wait()
-        prev = jnp.zeros((8, 128), F32)
-        for k in range(NL):
-            al = a_s[k]
-            below = al * sv[k]
-            above = al * sv[k + 1] if k + 1 < NL else jnp.zeros((8, 128), F32)
-            ip = 1.0 / (1.0 + below + above + below * prev)
-            prev = -above * ip
-            rat[k] = prev
-            inv[k] = ip
-            qq[k] = below * ip
-
         wait_all(mcp, esem.at[0])
         wait_all(mcn, esem.at[1])
         mch = jnp.where(sub >= 4, mcp[...], mcn[...])
         mch = jnp.where(valid, mch, 0.0)
         fh[...] = (-mch[None] * factors(halo(cut_s), halo(msk_s))).reshape(128, 128)
-        wait_all(eul, esem.at[2])
-        wait_all(eur, esem.at[3])
-        wait_all(ev.at[:, 7:8], esem.at[4])
-        wait_all(ev.at[:, 0:1], esem.at[5])
-        el, er = eul[...], eur[...]
-        for k in range(NL):
-            uk, vk = uv[k], vv[k]
-            evk = jnp.where(valid, ev[k], 0.0)
-            right = jnp.where(lane == 127, pltpu.roll(er, (95 - k) % 128, 1), pltpu.roll(uk, 127, 1))
-            left = jnp.where(lane == 0, pltpu.roll(el, (128 - k) % 128, 1), pltpu.roll(uk, 1, 1))
-            north = pltpu.roll(jnp.where(sub == 0, evk, vk), 7, 0)
-            south = pltpu.roll(jnp.where(sub == 7, evk, vk), 1, 0)
-            div0[k] = zc * (right - left) + mc * (north - south)
-    loads[4].wait()
     loads[5].wait()
     loads[6].wait()
 
@@ -272,50 +247,90 @@
         res[t * 128 : t * 128 + 128, :] = big_dot(turned)
         return unfold(t)
 
+    def zonal_part(ph, fa):
+        for d in range(16):
+            for l in range(2):
+                x, nx, pv_ = fa[d][l], fa[(d + 1) % 16][l], fa[(d + 15) % 16][l]
+                r2 = pltpu.roll(jnp.where(lane < 2, nx, x), 126, 1)
+                l2 = pltpu.roll(jnp.where(lane >= 126, pv_, x), 2, 1)
+                dsend[ph, d, l] = -zc * zc * ((r2 - x) - (x - l2))
+                if ph == SUBSTEPS - 1:
+                    r1 = pltpu.roll(jnp.where(lane < 1, nx, x), 127, 1)
+                    l1 = pltpu.roll(jnp.where(lane >= 127, pv_, x), 1, 1)
+                    du[d, l] = -zc * (r1 - l1)
+
+    def merid_spectra(own_spec, edge_spec):
+        wide = lax.broadcasted_iota(jnp.int32, (8, 256), 0)
+        bt, ht = [], []
+        for k1 in range(16):
+            o, e = own_spec[k1], edge_spec[k1]
+            ou, od = pltpu.roll(o, 7, 0), pltpu.roll(o, 1, 0)
+            eu_, ed_ = pltpu.roll(e, 7, 0), pltpu.roll(e, 1, 0)
+            bt.append(jnp.where(wide == 7, eu_, ou) - jnp.where(wide == 0, ed_, od))
+            ht.append(jnp.where(wide == 0, eu_ - od, ou - ed_))
+        return jnp.concatenate(bt, axis=0), jnp.concatenate(ht, axis=0)
+
+    def merid_part(ph, dy, hv):
+        for d in range(16):
+            for l in range(2):
+                x, e = dy[d][l], hv[d][l]
+                north = pltpu.roll(jnp.where(sub == 0, e, x), 7, 0)
+                south = pltpu.roll(jnp.where(sub == 7, e, x), 1, 0)
+                dsend[ph, d, l] = dsend[ph, d, l] + mc * (north - south)
+                if ph == SUBSTEPS - 1:
+                    dv[d, l] = x
+
+    def wait_edges(ph):
+        wait_all(xe.at[ph, :, :, 0:2], fesem.at[ph, 0])
+        wait_all(xe.at[ph, :, :, 0:2], fesem.at[ph, 1])
+
+    def fold_main(ph):
+        store_spec(0, dft16([(get_main(ph, d, 0), get_main(ph, d, 1)) for d in range(16)]))
+
+    def fold_edge(ph):
+        store_spec(1, dft16([(get_edge(ph, d, 0), get_edge(ph, d, 1)) for d in range(16)]))
+
+    def whole(ph):
+        fold_main(ph)
+        fold_edge(ph)
+        spec = big_dot(lhs[...])
+        bt, ht = merid_spectra(spec[0:128].reshape(16, 8, 256), spec[128:256].reshape(16, 8, 256))
+        fa = filtered(0, spec[0:128], fo)
+        hv = filtered(2, ht, fh)
+        dy = filtered(1, bt, fb)
+        zonal_part(ph, fa)
+        merid_part(ph, dy, hv)
+
+    def parted(ph):
+        fold_main(ph)
+        spec = big_dot(lhs[0:128, :])
+        zonal_part(ph, filtered(0, spec, fo))
+        if ph == SUBSTEPS - 1:
+            backward(du, ru, 12, bksem.at[2])
+        with jax.named_scope("waite%d" % ph):
+            wait_edges(ph)
+        with jax.named_scope("edge%d" % ph):
+            fold_edge(ph)
+            bt, ht = merid_spectra(spec.reshape(16, 8, 256), big_dot(lhs[128:256, :]).reshape(16, 8, 256))
+            hv = filtered(2, ht, fh)
+            dy = filtered(1, bt, fb)
+            merid_part(ph, dy, hv)
+
     def level_part(ph):
         with jax.named_scope("waitm%d" % ph):
             wait15(xm.at[ph], fmsem.at[ph])
-        with jax.named_scope("main%d" % ph):
-            store_spec(0, dft16([(get_main(ph, d, 0), get_main(ph, d, 1)) for d in range(16)]))
-            spec = big_dot(lhs[0:128, :])
-            own_spec = spec.reshape(16, 8, 256)
-            fa = filtered(0, spec, fo)
-            for d in range(16):
-                for l in range(2):
-                    x, nx, pv_ = fa[d][l], fa[(d + 1) % 16][l], fa[(d + 15) % 16][l]
-                    r2 = pltpu.roll(jnp.where(lane < 2, nx, x), 126, 1)
-                    l2 = pltpu.roll(jnp.where(lane >= 126, pv_, x), 2, 1)
-                    dsend[ph, d, l] = -zc * zc * ((r2 - x) - (x - l2))
-                    if ph == SUBSTEPS - 1:
-                        r1 = pltpu.roll(jnp.where(lane < 1, nx, x), 127, 1)
-                        l1 = pltpu.roll(jnp.where(lane >= 127, pv_, x), 1, 1)
-                        du[d, l] = -zc * (r1 - l1)
+
+        @pl.when(par == 0)
+        def _():
+            wait_edges(ph)
+            with jax.named_scope("whole%d" % ph):
+                whole(ph)
             if ph == SUBSTEPS - 1:
                 backward(du, ru, 12, bksem.at[2])
-        with jax.named_scope("waite%d" % ph):
-            wait_all(xe.at[ph, :, :, 0:2], fesem.at[ph, 0])
-            wait_all(xe.at[ph, :, :, 0:2], fesem.at[ph, 1])
-        with jax.named_scope("edge%d" % ph):
-            store_spec(1, dft16([(get_edge(ph, d, 0), get_edge(ph, d, 1)) for d in range(16)]))
-            edge_spec = big_dot(lhs[128:256, :]).reshape(16, 8, 256)
-            wide = lax.broadcasted_iota(jnp.int32, (8, 256), 0)
-            bt, ht = [], []
-            for k1 in range(16):
-                o, e = own_spec[k1], edge_spec[k1]
-                ou, od = pltpu.roll(o, 7, 0), pltpu.roll(o, 1, 0)
-                eu_, ed_ = pltpu.roll(e, 7, 0), pltpu.roll(e, 1, 0)
-                bt.append(jnp.where(wide == 7, eu_, ou) - jnp.where(wide == 0, ed_, od))
-                ht.append(jnp.where(wide == 0, eu_ - od, ou - ed_))
-            hv = filtered(2, jnp.concatenate(ht, axis=0), fh)
-            dy = filtered(1, jnp.concatenate(bt, axis=0), fb)
-            for d in range(16):
-                for l in range(2):
-                    x, e = dy[d][l], hv[d][l]
-                    north = pltpu.roll(jnp.where(sub == 0, e, x), 7, 0)
-                    south = pltpu.roll(jnp.where(sub == 7, e, x), 1, 0)
-                    dsend[ph, d, l] = dsend[ph, d, l] + mc * (north - south)
-                    if ph == SUBSTEPS - 1:
-                        dv[d, l] = x
+
+        @pl.when(par == 1)
+        def _():
+            parted(ph)
 
     def column(ph, pin, win, pout, wout):
         ps = [pin[k] - sv[k] * (div0[k] + back[ph, k]) for k in range(NL)]
@@ -342,6 +357,33 @@
     level_part(0)
     with jax.named_scope("bk0"):
         backward(dsend.at[0], back.at[0], 10, bksem.at[0])
+    with jax.named_scope("home2"):
+        loads[3].wait()
+        prev = jnp.zeros((8, 128), F32)
+        for k in range(NL):
+            al = a_s[k]
+            below = al * sv[k]
+            above = al * sv[k + 1] if k + 1 < NL else jnp.zeros((8, 128), F32)
+            ip = 1.0 / (1.0 + below + above + below * prev)
+            prev = -above * ip
+            rat[k] = prev
+            inv[k] = ip
+            qq[k] = below * ip
+
+        wait_all(eul, esem.at[2])
+        wait_all(eur, esem.at[3])
+        wait_all(ev.at[:, 7:8], esem.at[4])
+        wait_all(ev.at[:, 0:1], esem.at[5])
+        el, er = eul[...], eur[...]
+        for k in range(NL):
+            uk, vk = uv[k], vv[k]
+            evk = jnp.where(valid, ev[k], 0.0)
+            right = jnp.where(lane == 127, pltpu.roll(er, (95 - k) % 128, 1), pltpu.roll(uk, 127, 1))
+            left = jnp.where(lane == 0, pltpu.roll(el, (128 - k) % 128, 1), pltpu.roll(uk, 1, 1))
+            north = pltpu.roll(jnp.where(sub == 0, evk, vk), 7, 0)
+            south = pltpu.roll(jnp.where(sub == 7, evk, vk), 1, 0)
+            div0[k] = zc * (right - left) + mc * (north - south)
+        loads[4].wait()
     with jax.named_scope("waitb0"):
         wait30(back.at[0], bksem.at[0])
     with jax.named_scope("col0"):

time: 34.2 us -> 33.6 us (0.982)
  Pallas kernels: 33.4 us -> 32.8 us
    pallas_call x1, Pallas kernels: 32.6 us -> 32 us  [hold(): call(*xs)]
where the time goes in v4:
time: 33.6 us; the launch traced here: 33.4 us
  Pallas kernels  32.8 us (98%)
  between operations  0.64 us (2%)
    pallas_call x1, Pallas kernels, hold(): call(*xs)  32 us
    pallas_call x1, Pallas kernels, body(): finish(*hold(zc, mc, a, cutoff, mask, u, v, w, p, s, jnp.asarray(mat_np),...  0.82 us

profile of v4, /device:TPU:0, one launch (start us, length us, event | category | flops | bytes accessed | tf_op | source)
XLA Modules:
  0.0 33.4 jit_solution(9776895611673504020)
XLA Ops:
  0.6 32.0 %shard_map.147 = (f32[32,8,128]{2,1,0:T(8,128)S(1)}, f32[32,8,128]{2,1,0:T(8,128)S(1)}, f32[32,8,128]{2,1,0:T(8,128)S(1)}, f32[32,8,128]{2,1,0:T(8,128)S(1)}) custom-call(f32[8]{0:T(128)} %zc_h.1, f32[8]{0:T(128)} %mc_h.1, f32[32]{0:T(128)} %a_h.1, s32[64]{0:T(128)} %cut_h.1, s32[64]{0:T(128)} %msk_h.1, f32[32,8,128]{2,1,0:T(8,128)} %u_h.1, ...), custom_call_target="tpu_custom_call" | custom-call | tf_op jit(solution)/shard_map/pallas_call | solution.py:461
  32.6 0.8 %shard_map.148 = (f32[32,8,128]{2,1,0:T(8,128)}, f32[32,8,128]{2,1,0:T(8,128)}, f32[32,8,128]{2,1,0:T(8,128)}, f32[32,8,128]{2,1,0:T(8,128)}) custom-call(f32[32,8,128]{2,1,0:T(8,128)S(1)} %get-tuple-element.8.u, f32[32,8,128]{2,1,0:T(8,128)S(1)} %get-tuple-element.9.v, f32[32,8,128]{2,1,0:T(8,128)S(1)} %get-tuple-element.10.w, ...), custom_call_target="tpu_custom_call" | custom-call | tf_op jit(solution)/shard_map/pallas_call | solution.py:464

commit v5 on v4

--- a/solution.py
+++ b/solution.py
@@ -25,7 +25,8 @@
     low = (mat - high.astype(np.float64)).astype(np.float32).astype(jnp.bfloat16)
     mat = np.concatenate([high, high, low])
     tang = 2.0 * np.pi * (np.arange(16)[:, None] * lane[None, :]) / 2048.0
-    tw = np.stack([np.cos(tang), -np.sin(tang)]).astype(np.float32)
+    theta = 2.0 * np.pi * (np.arange(16)[:, None] + 16 * lane[None, :]) / 2048.0
+    tw = np.stack([np.cos(tang), -np.sin(tang), 2.0 * np.sin(theta)]).astype(np.float32)
     return mat, tw
 
 
@@ -73,7 +74,7 @@
     zc_h, mc_h, a_h, cut_h, msk_h, u_h, v_h, w_h, p_h, s_h, mat_h, tw_h,
     uo, vo, w2, p2,
     uv, vv, wv, pv, sv, mat, tw, p1, w1, xm, xe, lhs, res, dsend, back,
-    du, dv, ru, rv, rat, inv, qq, div0, eu, eul, eur, ev, mct, mcp, mcn, fo, fb, fh,
+    du, dv, ru, rv, rat, inv, qq, div0, eu, eul, eur, ev, mct, mcp, mcn, fo, fb, fd, fn, fs,
     zc_s, mc_s, a_s, cut_s, msk_s,
     ldsem, smsem, sendsem, fmsem, fesem, bksem, esem,
 ):
@@ -189,17 +190,28 @@
             damped = jnp.logical_and(kk > c, mask[None] > 0)
             return jnp.where(damped, ratio * ratio, 1.0) * (1.0 / 2048.0)
 
-        fo[...] = factors(own(cut_s), own(msk_s)).reshape(128, 128)
-        fb[...] = (-mc[None] * factors(own(cut_s), own(msk_s))).reshape(128, 128)
+        loads[5].wait()
+        loads[6].wait()
+        plain = factors(own(cut_s), own(msk_s))
+        fb[...] = (-mc[None] * plain).reshape(128, 128)
+        for k1 in range(16):
+            wave = zc * tw[2, k1 : k1 + 1, :]
+            fo[k1 * 8 : k1 * 8 + 8, :] = -wave * plain[k1]
+            fd[k1 * 8 : k1 * 8 + 8, :] = wave * wave * plain[k1]
 
         wait_all(mcp, esem.at[0])
         wait_all(mcn, esem.at[1])
         mch = jnp.where(sub >= 4, mcp[...], mcn[...])
         mch = jnp.where(valid, mch, 0.0)
-        fh[...] = (-mch[None] * factors(halo(cut_s), halo(msk_s))).reshape(128, 128)
-    loads[5].wait()
-    loads[6].wait()
-
+        rim = -mch[None] * factors(halo(cut_s), halo(msk_s))
+        for k1 in range(16):
+            row = slice(k1 * 8, k1 * 8 + 8)
+            b = fb[row, :]
+            above = mc * pltpu.roll(jnp.where(sub == 0, rim[k1], b), 7, 0)
+            below = mc * pltpu.roll(jnp.where(sub == 7, rim[k1], b), 1, 0)
+            fn[row, :] = above
+            fs[row, :] = below
+            fd[row, :] = fd[row, :] - (above + below)
     def get_main(ph, d, l):
         x = xm[0, d, l]
         return x + xm[1, d, l] if ph else x
@@ -207,7 +219,7 @@
     def get_edge(ph, d, l):
         x = xe[0, d, l]
         x = x + xe[1, d, l] if ph else x
-        return jnp.where(valid, x, 0.0)
+        return x
 
     def store_spec(t, spec):
         for k1 in range(16):
@@ -242,43 +254,55 @@
     def wait30(buf, sem):
         pltpu.make_async_copy(buf.at[pl.ds(0, 30)], buf.at[pl.ds(0, 30)], sem).wait()
 
-    def filtered(t, spec, f):
-        turned = jnp.concatenate([spec[:, 128:256] * f[...], spec[:, 0:128] * f[...]], axis=1)
-        res[t * 128 : t * 128 + 128, :] = big_dot(turned)
+    def inverse(t, real, imag):
+        res[t * 128 : t * 128 + 128, :] = big_dot(jnp.concatenate([imag, real], axis=1))
         return unfold(t)
 
-    def zonal_part(ph, fa):
+    def zonal(spec):
+        y = inverse(0, -(spec[:, 128:256] * fo[...]), spec[:, 0:128] * fo[...])
         for d in range(16):
             for l in range(2):
-                x, nx, pv_ = fa[d][l], fa[(d + 1) % 16][l], fa[(d + 15) % 16][l]
-                r2 = pltpu.roll(jnp.where(lane < 2, nx, x), 126, 1)
-                l2 = pltpu.roll(jnp.where(lane >= 126, pv_, x), 2, 1)
-                dsend[ph, d, l] = -zc * zc * ((r2 - x) - (x - l2))
-                if ph == SUBSTEPS - 1:
-                    r1 = pltpu.roll(jnp.where(lane < 1, nx, x), 127, 1)
-                    l1 = pltpu.roll(jnp.where(lane >= 127, pv_, x), 1, 1)
-                    du[d, l] = -zc * (r1 - l1)
-
-    def merid_spectra(own_spec, edge_spec):
-        wide = lax.broadcasted_iota(jnp.int32, (8, 256), 0)
-        bt, ht = [], []
-        for k1 in range(16):
-            o, e = own_spec[k1], edge_spec[k1]
-            ou, od = pltpu.roll(o, 7, 0), pltpu.roll(o, 1, 0)
-            eu_, ed_ = pltpu.roll(e, 7, 0), pltpu.roll(e, 1, 0)
-            bt.append(jnp.where(wide == 7, eu_, ou) - jnp.where(wide == 0, ed_, od))
-            ht.append(jnp.where(wide == 0, eu_ - od, ou - ed_))
-        return jnp.concatenate(bt, axis=0), jnp.concatenate(ht, axis=0)
-
-    def merid_part(ph, dy, hv):
+                du[d, l] = y[d][l]
+
+    def merid(real, imag):
+        y = inverse(1, real, imag)
         for d in range(16):
             for l in range(2):
-                x, e = dy[d][l], hv[d][l]
-                north = pltpu.roll(jnp.where(sub == 0, e, x), 7, 0)
-                south = pltpu.roll(jnp.where(sub == 7, e, x), 1, 0)
-                dsend[ph, d, l] = dsend[ph, d, l] + mc * (north - south)
-                if ph == SUBSTEPS - 1:
-                    dv[d, l] = x
+                dv[d, l] = y[d][l]
+
+    def diverge(ph, real, imag):
+        y = inverse(2, real, imag)
+        for d in range(16):
+            for l in range(2):
+                dsend[ph, d, l] = y[d][l]
+
+    def div_spectra(own_spec, edge_spec):
+        parts = []
+        for half in (0, 128):
+            out = []
+            for k1 in range(16):
+                row = slice(k1 * 8, k1 * 8 + 8)
+                o, e = own_spec[row, half : half + 128], edge_spec[row, half : half + 128]
+                e = jnp.where(valid, e, 0.0)
+                north = pltpu.roll(jnp.where(sub < 2, e, o), 6, 0)
+                south = pltpu.roll(jnp.where(sub >= 6, e, o), 2, 0)
+                out.append(fd[row, :] * o + fn[row, :] * north + fs[row, :] * south)
+            parts.append(jnp.concatenate(out, axis=0))
+        return parts
+
+    def dv_spectra(own_spec, edge_spec):
+        parts = []
+        for half in (0, 128):
+            out = []
+            for k1 in range(16):
+                row = slice(k1 * 8, k1 * 8 + 8)
+                o, e = own_spec[row, half : half + 128], edge_spec[row, half : half + 128]
+                e = jnp.where(valid, e, 0.0)
+                north = pltpu.roll(jnp.where(sub == 0, e, o), 7, 0)
+                south = pltpu.roll(jnp.where(sub == 7, e, o), 1, 0)
+                out.append(fb[row, :] * (north - south))
+            parts.append(jnp.concatenate(out, axis=0))
+        return parts
 
     def wait_edges(ph):
         wait_all(xe.at[ph, :, :, 0:2], fesem.at[ph, 0])
@@ -289,32 +313,44 @@
 
     def fold_edge(ph):
         store_spec(1, dft16([(get_edge(ph, d, 0), get_edge(ph, d, 1)) for d in range(16)]))
+
+    def send_du():
+        backward(du, ru, 12, bksem.at[2])
+
+    def send_dv():
+        backward(dv, rv, 13, bksem.at[3])
+
+    def send_div(ph):
+        backward(dsend.at[ph], back.at[ph], 10 + ph, bksem.at[ph])
 
     def whole(ph):
         fold_main(ph)
         fold_edge(ph)
         spec = big_dot(lhs[...])
-        bt, ht = merid_spectra(spec[0:128].reshape(16, 8, 256), spec[128:256].reshape(16, 8, 256))
-        fa = filtered(0, spec[0:128], fo)
-        hv = filtered(2, ht, fh)
-        dy = filtered(1, bt, fb)
-        zonal_part(ph, fa)
-        merid_part(ph, dy, hv)
+        diverge(ph, *div_spectra(spec[0:128], spec[128:256]))
+        send_div(ph)
+        if ph == SUBSTEPS - 1:
+            zonal(spec[0:128])
+            send_du()
+            merid(*dv_spectra(spec[0:128], spec[128:256]))
+            send_dv()
 
     def parted(ph):
         fold_main(ph)
         spec = big_dot(lhs[0:128, :])
-        zonal_part(ph, filtered(0, spec, fo))
         if ph == SUBSTEPS - 1:
-            backward(du, ru, 12, bksem.at[2])
+            zonal(spec)
+            send_du()
         with jax.named_scope("waite%d" % ph):
             wait_edges(ph)
         with jax.named_scope("edge%d" % ph):
             fold_edge(ph)
-            bt, ht = merid_spectra(spec.reshape(16, 8, 256), big_dot(lhs[128:256, :]).reshape(16, 8, 256))
-            hv = filtered(2, ht, fh)
-            dy = filtered(1, bt, fb)
-            merid_part(ph, dy, hv)
+            edge_spec = big_dot(lhs[128:256, :])
+            diverge(ph, *div_spectra(spec, edge_spec))
+            send_div(ph)
+            if ph == SUBSTEPS - 1:
+                merid(*dv_spectra(spec, edge_spec))
+                send_dv()
 
     def level_part(ph):
         with jax.named_scope("waitm%d" % ph):
@@ -325,8 +361,6 @@
             wait_edges(ph)
             with jax.named_scope("whole%d" % ph):
                 whole(ph)
-            if ph == SUBSTEPS - 1:
-                backward(du, ru, 12, bksem.at[2])
 
         @pl.when(par == 1)
         def _():
@@ -355,8 +389,6 @@
                 pout[k] = ps[k] - sv[k] * wk
 
     level_part(0)
-    with jax.named_scope("bk0"):
-        backward(dsend.at[0], back.at[0], 10, bksem.at[0])
     with jax.named_scope("home2"):
         loads[3].wait()
         prev = jnp.zeros((8, 128), F32)
@@ -391,9 +423,6 @@
     with jax.named_scope("fwd1"):
         forward(1, p1)
     level_part(1)
-    with jax.named_scope("bk1"):
-        backward(dsend.at[1], back.at[1], 11, bksem.at[1])
-        backward(dv, rv, 13, bksem.at[3])
     with jax.named_scope("waitb1"):
         wait30(back.at[1], bksem.at[1])
     with jax.named_scope("col1"):
@@ -436,11 +465,11 @@
     rows = pltpu.VMEM((384, 256), F32)
     dma = pltpu.SemaphoreType.DMA
     scratch = [
-        blk, blk, blk, blk, blk, pltpu.VMEM((768, 256), jnp.bfloat16), pltpu.VMEM((2, 16, 128), F32),
+        blk, blk, blk, blk, blk, pltpu.VMEM((768, 256), jnp.bfloat16), pltpu.VMEM((3, 16, 128), F32),
         blk, blk, quad, quad, pltpu.VMEM((256, 256), F32), rows, quad, pltpu.VMEM((2, NL, 8, 128), F32),
         pltpu.VMEM((16, 2, 8, 128), F32), pltpu.VMEM((16, 2, 8, 128), F32), blk, blk,
         blk, blk, blk, blk, line, line, line, blk, line, line, line,
-        pltpu.VMEM((128, 128), F32), pltpu.VMEM((128, 128), F32), pltpu.VMEM((128, 128), F32),
+        pltpu.VMEM((128, 128), F32), pltpu.VMEM((128, 128), F32), pltpu.VMEM((128, 128), F32), pltpu.VMEM((128, 128), F32), pltpu.VMEM((128, 128), F32),
         pltpu.SMEM((8,), F32), pltpu.SMEM((8,), F32), pltpu.SMEM((NL,), F32), pltpu.SMEM((64,), jnp.int32), pltpu.SMEM((64,), jnp.int32),
         dma((7,)), dma((5,)), dma((14,)), dma((2,)), dma((2, 2)), dma((4,)), dma((6,)),
     ]

time: 33.6 us -> 33.3 us (level)
  no operation moved by 1% of the time
where the time goes in v5:
time: 33.3 us; the launch traced here: 33.1 us
  Pallas kernels  32.5 us (98%)
  between operations  0.64 us (2%)
    pallas_call x1, Pallas kernels, hold(): call(*xs)  31.7 us
    pallas_call x1, Pallas kernels, body(): finish(*hold(zc, mc, a, cutoff, mask, u, v, w, p, s, jnp.asarray(mat_np),...  0.82 us

profile of v5, /device:TPU:0, one launch (start us, length us, event | category | flops | bytes accessed | tf_op | source)
XLA Modules:
  0.0 33.1 jit_solution(12754850233555706291)
XLA Ops:
  0.6 31.7 %shard_map.147 = (f32[32,8,128]{2,1,0:T(8,128)S(1)}, f32[32,8,128]{2,1,0:T(8,128)S(1)}, f32[32,8,128]{2,1,0:T(8,128)S(1)}, f32[32,8,128]{2,1,0:T(8,128)S(1)}) custom-call(f32[8]{0:T(128)} %zc_h.1, f32[8]{0:T(128)} %mc_h.1, f32[32]{0:T(128)} %a_h.1, s32[64]{0:T(128)} %cut_h.1, s32[64]{0:T(128)} %msk_h.1, f32[32,8,128]{2,1,0:T(8,128)} %u_h.1, ...), custom_call_target="tpu_custom_call" | custom-call | tf_op jit(solution)/shard_map/pallas_call | solution.py:490
  32.3 0.8 %shard_map.148 = (f32[32,8,128]{2,1,0:T(8,128)}, f32[32,8,128]{2,1,0:T(8,128)}, f32[32,8,128]{2,1,0:T(8,128)}, f32[32,8,128]{2,1,0:T(8,128)}) custom-call(f32[32,8,128]{2,1,0:T(8,128)S(1)} %get-tuple-element.8.u, f32[32,8,128]{2,1,0:T(8,128)S(1)} %get-tuple-element.9.v, f32[32,8,128]{2,1,0:T(8,128)S(1)} %get-tuple-element.10.w, ...), custom_call_target="tpu_custom_call" | custom-call | tf_op jit(solution)/shard_map/pallas_call | solution.py:493

commit v6 on v5

--- a/solution.py
+++ b/solution.py
@@ -76,7 +76,7 @@
     uv, vv, wv, pv, sv, mat, tw, p1, w1, xm, xe, lhs, res, dsend, back,
     du, dv, ru, rv, rat, inv, qq, div0, eu, eul, eur, ev, mct, mcp, mcn, fo, fb, fd, fn, fs,
     zc_s, mc_s, a_s, cut_s, msk_s,
-    ldsem, smsem, sendsem, fmsem, fesem, bksem, esem,
+    ldsem, smsem, sendsem, fmsem, fesem, bksem, esem, ready,
 ):
     me = lax.axis_index("lon")
     g = lax.axis_index("lat")
@@ -104,13 +104,14 @@
     def target(off):
         return ((my + off[0]) % 4) * 4 + (mx + off[1]) % 4
 
+    def tell(sem, gg, d):
+        pl.semaphore_signal(sem, inc=1, device_id={"lat": gg, "lon": d}, device_id_type=MESH)
+
     for off in OFFS:
-        d = target(off)
-        pl.semaphore_signal(bar, inc=1, device_id={"lat": up, "lon": d}, device_id_type=MESH)
-        pl.semaphore_signal(bar, inc=1, device_id={"lat": dn, "lon": d}, device_id_type=MESH)
         if off != (0, 0):
-            pl.semaphore_signal(bar, inc=1, device_id={"lat": g, "lon": d}, device_id_type=MESH)
-
+            tell(bar, g, target(off))
+    tell(bar, up, me)
+    tell(bar, dn, me)
     for c in loads[:1] + small + loads[1:]:
         c.start()
 
@@ -121,11 +122,13 @@
         )
         c.start()
 
-    def forward(ph, src):
+    def send_edges(ph, src):
         for off in OFFS:
             d = target(off)
             rcopy(src.at[pl.ds(2 * d, 2), 6:8], xe.at[ph, me, :, 6:8], 3 * ph + 1, fesem.at[ph, 0], up, d)
             rcopy(src.at[pl.ds(2 * d, 2), 0:2], xe.at[ph, me, :, 0:2], 3 * ph + 2, fesem.at[ph, 1], dn, d)
+
+    def send_main(ph, src):
         for off in OFFS:
             d = target(off)
             if off != (0, 0):
@@ -161,11 +164,13 @@
         mct[...] = mc
         own = lambda ref: tile(lambda r: ref[8 * g + r])
         halo = lambda ref: jnp.where(sub == 0, ref[(8 * g + 8) % 64], ref[(8 * g + 63) % 64])
-        pl.semaphore_wait(bar, 47)
+        pl.semaphore_wait(bar, 17)
+        tell(ready, up, me)
+        tell(ready, dn, me)
     with jax.named_scope("fwd0"):
         rcopy(mct, mcp, 6, esem.at[0], up, me)
         rcopy(mct, mcn, 6, esem.at[1], dn, me)
-        forward(0, pv)
+        send_main(0, pv)
     with jax.named_scope("home"):
         loads[1].wait()
         e = jnp.zeros((8, 128), F32)
@@ -174,6 +179,8 @@
             e = jnp.where(lane == k, pltpu.roll(uk, (k + 1) % 128, 1), e)
             e = jnp.where(lane == 32 + k, pltpu.roll(uk, 32 + k, 1), e)
         eu[...] = e
+        pl.semaphore_wait(ready, 2)
+        send_edges(0, pv)
         rcopy(eu, eul, 7, esem.at[2], g, east)
         rcopy(eu, eur, 7, esem.at[3], g, west)
         loads[2].wait()
@@ -355,6 +362,10 @@
     def level_part(ph):
         with jax.named_scope("waitm%d" % ph):
             wait15(xm.at[ph], fmsem.at[ph])
+
+        if ph == 0:
+            parted(ph)
+            return
 
         @pl.when(par == 0)
         def _():
@@ -421,7 +432,8 @@
     with jax.named_scope("col0"):
         column(0, pv, wv, p1, w1)
     with jax.named_scope("fwd1"):
-        forward(1, p1)
+        send_edges(1, p1)
+        send_main(1, p1)
     level_part(1)
     with jax.named_scope("waitb1"):
         wait30(back.at[1], bksem.at[1])
@@ -471,7 +483,7 @@
         blk, blk, blk, blk, line, line, line, blk, line, line, line,
         pltpu.VMEM((128, 128), F32), pltpu.VMEM((128, 128), F32), pltpu.VMEM((128, 128), F32), pltpu.VMEM((128, 128), F32), pltpu.VMEM((128, 128), F32),
         pltpu.SMEM((8,), F32), pltpu.SMEM((8,), F32), pltpu.SMEM((NL,), F32), pltpu.SMEM((64,), jnp.int32), pltpu.SMEM((64,), jnp.int32),
-        dma((7,)), dma((5,)), dma((14,)), dma((2,)), dma((2, 2)), dma((4,)), dma((6,)),
+        dma((7,)), dma((5,)), dma((14,)), dma((2,)), dma((2, 2)), dma((4,)), dma((6,)), pltpu.SemaphoreType.REGULAR,
     ]
     call = pl.pallas_call(
         kernel,

time: 33.3 us -> 33.1 us (level)
  no operation moved by 1% of the time
where the time goes in v6:
time: 33.1 us; the launch traced here: 33 us
  Pallas kernels  32.3 us (98%)
  between operations  0.64 us (2%)
    pallas_call x1, Pallas kernels, hold(): call(*xs)  31.5 us
    pallas_call x1, Pallas kernels, body(): finish(*hold(zc, mc, a, cutoff, mask, u, v, w, p, s, jnp.asarray(mat_np),...  0.82 us

profile of v6, /device:TPU:0, one launch (start us, length us, event | category | flops | bytes accessed | tf_op | source)
XLA Modules:
  0.0 33.0 jit_solution(16480583957981140999)
XLA Ops:
  0.6 31.5 %shard_map.147 = (f32[32,8,128]{2,1,0:T(8,128)S(1)}, f32[32,8,128]{2,1,0:T(8,128)S(1)}, f32[32,8,128]{2,1,0:T(8,128)S(1)}, f32[32,8,128]{2,1,0:T(8,128)S(1)}) custom-call(f32[8]{0:T(128)} %zc_h.1, f32[8]{0:T(128)} %mc_h.1, f32[32]{0:T(128)} %a_h.1, s32[64]{0:T(128)} %cut_h.1, s32[64]{0:T(128)} %msk_h.1, f32[32,8,128]{2,1,0:T(8,128)} %u_h.1, ...), custom_call_target="tpu_custom_call" | custom-call | tf_op jit(solution)/shard_map/pallas_call | solution.py:502
  32.1 0.8 %shard_map.148 = (f32[32,8,128]{2,1,0:T(8,128)}, f32[32,8,128]{2,1,0:T(8,128)}, f32[32,8,128]{2,1,0:T(8,128)}, f32[32,8,128]{2,1,0:T(8,128)}) custom-call(f32[32,8,128]{2,1,0:T(8,128)S(1)} %get-tuple-element.8.u, f32[32,8,128]{2,1,0:T(8,128)S(1)} %get-tuple-element.9.v, f32[32,8,128]{2,1,0:T(8,128)S(1)} %get-tuple-element.10.w, ...), custom_call_target="tpu_custom_call" | custom-call | tf_op jit(solution)/shard_map/pallas_call | solution.py:505

commit v7 on v6

--- a/solution.py
+++ b/solution.py
@@ -122,11 +122,38 @@
         )
         c.start()
 
+    def edge_up(ph, src, d):
+        rcopy(src.at[pl.ds(2 * d, 2), 6:8], xe.at[ph, me, :, 6:8], 3 * ph + 1, fesem.at[ph, 0], up, d)
+
+    def edge_dn(ph, src, d):
+        rcopy(src.at[pl.ds(2 * d, 2), 0:2], xe.at[ph, me, :, 0:2], 3 * ph + 2, fesem.at[ph, 1], dn, d)
+
     def send_edges(ph, src):
         for off in OFFS:
             d = target(off)
-            rcopy(src.at[pl.ds(2 * d, 2), 6:8], xe.at[ph, me, :, 6:8], 3 * ph + 1, fesem.at[ph, 0], up, d)
-            rcopy(src.at[pl.ds(2 * d, 2), 0:2], xe.at[ph, me, :, 0:2], 3 * ph + 2, fesem.at[ph, 1], dn, d)
+            edge_up(ph, src, d)
+            edge_dn(ph, src, d)
+
+    def first_edges(src):
+        def ups():
+            pl.semaphore_wait(ready.at[1], 1)
+            for off in OFFS:
+                edge_up(0, src, target(off))
+
+        def downs():
+            pl.semaphore_wait(ready.at[0], 1)
+            for off in OFFS:
+                edge_dn(0, src, target(off))
+
+        @pl.when(par == 0)
+        def _():
+            ups()
+            downs()
+
+        @pl.when(par == 1)
+        def _():
+            downs()
+            ups()
 
     def send_main(ph, src):
         for off in OFFS:
@@ -165,8 +192,8 @@
         own = lambda ref: tile(lambda r: ref[8 * g + r])
         halo = lambda ref: jnp.where(sub == 0, ref[(8 * g + 8) % 64], ref[(8 * g + 63) % 64])
         pl.semaphore_wait(bar, 17)
-        tell(ready, up, me)
-        tell(ready, dn, me)
+        tell(ready.at[0], up, me)
+        tell(ready.at[1], dn, me)
     with jax.named_scope("fwd0"):
         rcopy(mct, mcp, 6, esem.at[0], up, me)
         rcopy(mct, mcn, 6, esem.at[1], dn, me)
@@ -179,8 +206,7 @@
             e = jnp.where(lane == k, pltpu.roll(uk, (k + 1) % 128, 1), e)
             e = jnp.where(lane == 32 + k, pltpu.roll(uk, 32 + k, 1), e)
         eu[...] = e
-        pl.semaphore_wait(ready, 2)
-        send_edges(0, pv)
+        first_edges(pv)
         rcopy(eu, eul, 7, esem.at[2], g, east)
         rcopy(eu, eur, 7, esem.at[3], g, west)
         loads[2].wait()
@@ -483,7 +509,7 @@
         blk, blk, blk, blk, line, line, line, blk, line, line, line,
         pltpu.VMEM((128, 128), F32), pltpu.VMEM((128, 128), F32), pltpu.VMEM((128, 128), F32), pltpu.VMEM((128, 128), F32), pltpu.VMEM((128, 128), F32),
         pltpu.SMEM((8,), F32), pltpu.SMEM((8,), F32), pltpu.SMEM((NL,), F32), pltpu.SMEM((64,), jnp.int32), pltpu.SMEM((64,), jnp.int32),
-        dma((7,)), dma((5,)), dma((14,)), dma((2,)), dma((2, 2)), dma((4,)), dma((6,)), pltpu.SemaphoreType.REGULAR,
+        dma((7,)), dma((5,)), dma((14,)), dma((2,)), dma((2, 2)), dma((4,)), dma((6,)), pltpu.SemaphoreType.REGULAR((2,)),
     ]
     call = pl.pallas_call(
         kernel,

time: 33.1 us -> 33.1 us (level)
  no operation moved by 1% of the time
where the time goes in v7:
time: 33.1 us; the launch traced here: 33 us
  Pallas kernels  32.4 us (98%)
  between operations  0.64 us (2%)
    pallas_call x1, Pallas kernels, hold(): call(*xs)  31.6 us
    pallas_call x1, Pallas kernels, body(): finish(*hold(zc, mc, a, cutoff, mask, u, v, w, p, s, jnp.asarray(mat_np),...  0.82 us

profile of v7, /device:TPU:0, one launch (start us, length us, event | category | flops | bytes accessed | tf_op | source)
XLA Modules:
  0.0 33.0 jit_solution(1521026098972396499)
XLA Ops:
  0.6 31.6 %shard_map.147 = (f32[32,8,128]{2,1,0:T(8,128)S(1)}, f32[32,8,128]{2,1,0:T(8,128)S(1)}, f32[32,8,128]{2,1,0:T(8,128)S(1)}, f32[32,8,128]{2,1,0:T(8,128)S(1)}) custom-call(f32[8]{0:T(128)} %zc_h.1, f32[8]{0:T(128)} %mc_h.1, f32[32]{0:T(128)} %a_h.1, s32[64]{0:T(128)} %cut_h.1, s32[64]{0:T(128)} %msk_h.1, f32[32,8,128]{2,1,0:T(8,128)} %u_h.1, ...), custom_call_target="tpu_custom_call" | custom-call | tf_op jit(solution)/shard_map/pallas_call | solution.py:528
  32.2 0.8 %shard_map.148 = (f32[32,8,128]{2,1,0:T(8,128)}, f32[32,8,128]{2,1,0:T(8,128)}, f32[32,8,128]{2,1,0:T(8,128)}, f32[32,8,128]{2,1,0:T(8,128)}) custom-call(f32[32,8,128]{2,1,0:T(8,128)S(1)} %get-tuple-element.8.u, f32[32,8,128]{2,1,0:T(8,128)S(1)} %get-tuple-element.9.v, f32[32,8,128]{2,1,0:T(8,128)S(1)} %get-tuple-element.10.w, ...), custom_call_target="tpu_custom_call" | custom-call | tf_op jit(solution)/shard_map/pallas_call | solution.py:531
